TPU v7x, 32 devices: a whole 2x2x4 slice. The times are simulated.
32 devices in a mesh: shard: 8 (over z, core), rep: 4 (over y, x).
Axes of the slice: x: 2, y: 2, z: 4, core: 2. Of those that a mesh axis runs over, the one named last changes fastest.
Arguments:
- tokens: bfloat16 [12288, 5120], P(('shard', 'rep')), may hold values from -700 to 700
- norm_gain: float32 [5120], replicated, may hold values from 0.1 to 1.9
- key_bias: float32 [1024], replicated, may hold values from -4 to 4
- key_weight: bfloat16 [8192, 1024], P('shard'), may hold values from -0.078125 to 0.078125
- cotangent: bfloat16 [12288, 1024], P(('shard', 'rep')), may hold values from -40 to 40
- block_slot: int32 [40], replicated, may hold values from 0 to 63, as said below
Outputs:
- projected: bfloat16 [12288, 1024], P(('shard', 'rep'))
- token_grad: bfloat16 [12288, 5120], P(('shard', 'rep'))
- weight_grad: float32 [8192, 1024], P('shard')
- gain_grad: float32 [5120], replicated
- bias_grad: float32 [1024], replicated
Inputs may be any that keep to these rules, and one draw needn't show every extreme that they name: Entries are distinct; block b lies on the device of shard with index block_slot[b] // 8, at its local slot block_slot[b] % 8; in every draw some device holds 8 blocks.
All inputs are finite; a program needn't handle non-finite values.
Results may differ from a plain program's by a relative error of at most 0.013.
Values may be sent and summed in bfloat16 or wider, within the bound.
A program may use at most 128 MiB of HBM per device.

v0:
```python
import functools
import jax
import jax.numpy as jnp
from jax import lax
from jax.experimental import pallas as pl
from jax.experimental.pallas import tpu as pltpu
from jax.sharding import PartitionSpec as P

BLK = 128
EPS = 1e-06
NJ = 4
SUB = BLK // NJ
QUAD = 4
MESH = pl.DeviceIdType.MESH
F32 = jnp.float32
BF16 = jnp.bfloat16


def comm_kernel(
    planes, cap, nblk, scale,
    tok, gain, cot, bias, bos, slot_of, w, proj, tgrad, wgrad, vec,
    whole, inv, coef, fwd, gst, grecv, gz, part, drecv, r1, r2, slots, zup, zdn, fin, frecv,
    loc_sem, agz_s, agz_r, agx_s, agx_r, agy_s, agy_r, agp_s, agp_r,
    d_s, d_r, r1_s, r1_r, r2_s, r2_r, zu_s, zu_r, zd_s, zd_r, f_s, f_r, g_s, g_r, gz_s, gz_r,
):
    s = lax.axis_index("shard")
    r = lax.axis_index("rep")
    z = s // 2
    c = s % 2
    quad = r % QUAD
    base = r - quad
    y = quad // 2
    x = quad % 2
    xq = y * 2 + (1 - x)
    yq = (1 - y) * 2 + x
    dq = (1 - y) * 2 + (1 - x)
    oc = 1 - c
    partner = (2 * z + oc, r)
    xdev = (s, base + xq)
    ydev = (s, base + yq)
    updev = (s + 2, r)
    dndev = (s - 2, r)
    plane = [(2 * z + oc, r)]
    for q in (xq, yq, dq):
        for cc in (c, oc):
            plane.append((2 * z + cc, base + q))
    has_up = z < planes - 1
    has_dn = z > 0

    bar = pltpu.get_barrier_semaphore()
    for dev in plane:
        pl.semaphore_signal(bar, inc=1, device_id=dev, device_id_type=MESH)

    others = [(2 * ((z + d) % planes) + c, r) for d in range(1, planes)]
    for dev in others:
        pl.semaphore_signal(bar, inc=1, device_id=dev, device_id_type=MESH)
    pl.semaphore_wait(bar, 7 + planes - 1)

    def rdma(src, dst, ss, rs, dev):
        return pltpu.make_async_remote_copy(
            src_ref=src, dst_ref=dst, send_sem=ss, recv_sem=rs, device_id=dev, device_id_type=MESH
        )

    half = cap // 2
    quar = cap // 4
    hh = (x + y) % 2

    def span(shard, start, size):
        return whole.at[pl.ds(shard * cap + start, size)]

    mine = (hh * half, half)
    mine_x = (hh * half, quar)
    mine_y = (hh * half + quar, quar)
    other_x = ((1 - hh) * half, quar)
    other_y = ((1 - hh) * half + quar, quar)

    def own_z(d, dev):
        return rdma(w.at[pl.ds(*mine)], span(s, *mine), agz_s.at[d, z], agz_r.at[z], dev)

    def fwd_z(q, d, dev):
        ref = span(2 * q + c, *mine)
        return rdma(ref, ref, agz_s.at[d, q], agz_r.at[q], dev)

    def fwd_x(q):
        ref = span(2 * q + c, *mine_x)
        return rdma(ref, ref, agx_s.at[q], agx_r.at[q], xdev)

    def fwd_y(q):
        ref = span(2 * q + c, *mine_y)
        return rdma(ref, ref, agy_s.at[q], agy_r.at[q], ydev)

    def got_x(q):
        ref = span(2 * q + c, *other_x)
        return rdma(ref, ref, agx_s.at[q], agx_r.at[q], xdev)

    def got_y(q):
        ref = span(2 * q + c, *other_y)
        return rdma(ref, ref, agy_s.at[q], agy_r.at[q], ydev)

    def to_partner(i, q, rng):
        ref = span(2 * q + c, *rng)
        return rdma(ref, ref, agp_s.at[i, q], agp_r.at[i, q], partner)

    def from_partner(i, q, rng):
        ref = span(2 * q + oc, *rng)
        return rdma(ref, ref, agp_s.at[i, q], agp_r.at[i, q], partner)

    own_partner = rdma(w, span(s, 0, cap), agp_s.at[0, z], agp_r.at[0, z], partner)
    own_local = pltpu.make_async_copy(w, span(s, 0, cap), loc_sem)

    @pl.when(has_up)
    def _():
        own_z(0, updev).start()

    @pl.when(has_dn)
    def _():
        own_z(1, dndev).start()

    own_partner.start()
    own_local.start()

    def each_foreign(t, f):
        @pl.when(z - t >= 0)
        def _():
            f(z - t, 0)

        @pl.when(z + t < planes)
        def _():
            f(z + t, 1)

    def ag_arrive(t):
        def f(q, d):
            fwd_z(q, d, updev).wait_recv()
            if d == 0:
                @pl.when(has_up)
                def _():
                    fwd_z(q, 0, updev).start()
            else:
                @pl.when(has_dn)
                def _():
                    fwd_z(q, 1, dndev).start()
            fwd_x(q).start()
            fwd_y(q).start()
            to_partner(1, q, mine).start()

        each_foreign(t, f)

    def ag_side(t):
        def f(q, d):
            got_x(q).wait_recv()
            to_partner(2, q, other_x).start()
            got_y(q).wait_recv()
            to_partner(3, q, other_y).start()

        each_foreign(t, f)

    def ag_finish(t):
        def f(q, d):
            from_partner(1, q, mine).wait_recv()
            from_partner(2, q, other_x).wait_recv()
            from_partner(3, q, other_y).wait_recv()
            to_partner(1, q, mine).wait_send()
            to_partner(2, q, other_x).wait_send()
            to_partner(3, q, other_y).wait_send()
            fwd_x(q).wait_send()
            fwd_y(q).wait_send()
            if d == 0:
                @pl.when(has_up)
                def _():
                    fwd_z(q, 0, updev).wait_send()
            else:
                @pl.when(has_dn)
                def _():
                    fwd_z(q, 1, dndev).wait_send()

        each_foreign(t, f)

    tokens_here, width = tok.shape
    wide = 2 * BLK

    def squares(i, acc):
        v = tok[:, pl.ds(pl.multiple_of(i * wide, wide), wide)].astype(F32)
        v = v * v
        return acc + v[:, :BLK] + v[:, BLK:]

    acc = lax.fori_loop(0, width // wide, squares, jnp.zeros((tokens_here, BLK), F32))
    inv[...] = lax.rsqrt(jnp.sum(acc, axis=1, keepdims=True) / width + EPS)

    def term(i, carry):
        cols = pl.ds(pl.multiple_of(i * wide, wide), wide)
        normed = (tok[:, cols].astype(F32) * inv[...] * gain[:, cols]).astype(BF16)
        res = lax.dot_general(
            normed, cot[...], (((0,), (0,)), ((), ())), preferred_element_type=F32
        )
        res = (res * scale).astype(BF16)
        group = res.shape[1] // (2 * QUAD)
        for b in range(2):
            for j in range(NJ):
                lo = b * BLK + j * SUB
                for k in range(QUAD):
                    for cc in range(2):
                        col = (k * 2 + cc) * group
                        part[cc, j, k, i * 2 + b] = res[lo:lo + SUB, col:col + group]
        return carry


    hb = nblk // 2

    def d_copy(j, i):
        blocks = pl.ds(i * hb, hb)
        return rdma(
            part.at[oc, j, :, blocks], drecv.at[j, :, blocks], d_s.at[j, i], d_r.at[j, i], partner
        )

    for i in range(2):
        lax.fori_loop(i * hb // 2, (i + 1) * hb // 2, term, 0)
        for j in range(NJ):
            d_copy(j, i).start()

    def add_to(dst, src, count):
        step = 8

        def body(i, carry):
            sl = pl.ds(i * step, step)
            dst[sl] = (dst[sl].astype(F32) + src[sl].astype(F32)).astype(BF16)
            return carry

        lax.fori_loop(0, count // step, body, 0)

    def first_hop(j):
        near, dev = (xq, xdev) if j % 2 == 0 else (yq, ydev)
        return (
            rdma(part.at[c, j, near], r1.at[j, 0], r1_s.at[j, 0], r1_r.at[j, 0], dev),
            rdma(part.at[c, j, dq], r1.at[j, 1], r1_s.at[j, 1], r1_r.at[j, 1], dev),
        )

    def second_hop(j):
        far, dev = (yq, ydev) if j % 2 == 0 else (xq, xdev)
        return rdma(part.at[c, j, far], r2.at[j], r2_s.at[j], r2_r.at[j], dev)

    def core_sum(j):
        for i in range(2):
            d_copy(j, i).wait()
        for k in range(QUAD):
            add_to(part.at[c, j, k], drecv.at[j, k], nblk)

    def first_send(j):
        hops = first_hop(j)
        hops[1].start()
        hops[0].start()

    def second_send(j):
        hops = first_hop(j)
        far = yq if j % 2 == 0 else xq
        hops[1].wait_recv()
        add_to(part.at[c, j, far], r1.at[j, 1], nblk)
        second_hop(j).start()
        hops[0].wait_recv()
        add_to(part.at[c, j, quad], r1.at[j, 0], nblk)

    per_plane = 2 * cap

    def z_copy(buf, ss, rs, j, q, dev):
        return rdma(slots.at[j, q], buf.at[j, q], ss.at[j, q], rs.at[j, q], dev)

    def up_copy(j, q):
        return z_copy(zup, zu_s, zu_r, j, q, updev)

    def dn_copy(j, q):
        return z_copy(zdn, zd_s, zd_r, j, q, dndev)

    def place(j):
        second_hop(j).wait_recv()
        add_to(part.at[c, j, quad], r2.at[j], nblk)

        def body(i, carry):
            for u in range(per_plane):
                b = bos[i * per_plane + u]
                val = part[c, j, quad, jnp.maximum(b, 0)]
                slots[j, i, u] = jnp.where(b >= 0, val.astype(F32), 0.0).astype(BF16)
            return carry

        lax.fori_loop(0, planes, body, 0)

    def z_step(j, t):
        qu = planes - 1 - t

        @pl.when(z < qu)
        def _():
            @pl.when(has_dn)
            def _():
                up_copy(j, qu).wait_recv()
                add_to(slots.at[j, qu], zup.at[j, qu], per_plane)

            up_copy(j, qu).start()

        @pl.when(z > t)
        def _():
            @pl.when(has_up)
            def _():
                dn_copy(j, t).wait_recv()
                add_to(slots.at[j, t], zdn.at[j, t], per_plane)

            dn_copy(j, t).start()

    my_id = quad * 2 + c

    def f_copies(j):
        out = []
        for n, dev in enumerate(plane):
            cc = oc if n % 2 == 0 else c
            out.append(
                rdma(
                    fin.at[j, pl.ds(cc * cap, cap)], frecv.at[my_id, j],
                    f_s.at[j, n], f_r.at[j, my_id], dev,
                )
            )
        return out

    def z_end(j):
        @pl.when(has_dn)
        def _():
            up_copy(j, z).wait_recv()
            add_to(slots.at[j, z], zup.at[j, z], per_plane)

        @pl.when(has_up)
        def _():
            dn_copy(j, z).wait_recv()
            add_to(slots.at[j, z], zdn.at[j, z], per_plane)

        fin[j] = slots[j, z]
        frecv[my_id, j] = slots[j, z, pl.ds(c * cap, cap)]
        for cp in f_copies(j):
            cp.start()

    grp = 4
    gw = grp * BLK

    def weight_group(g):
        return jnp.concatenate([whole[slot_of[g * grp + i]] for i in range(grp)], axis=0)

    def fwd_body(g, carry):
        cols = pl.ds(pl.multiple_of(g * gw, gw), gw)
        normed = (tok[:, cols].astype(F32) * inv[...] * gain[:, cols]).astype(BF16)
        fwd[...] += jnp.dot(normed, weight_group(g), preferred_element_type=F32)
        return carry

    def bwd_body(g, carry):
        cols = pl.ds(pl.multiple_of(g * gw, gw), gw)
        grad = lax.dot_general(
            cot[...], weight_group(g), (((1,), (1,)), ((), ())), preferred_element_type=F32
        )
        values = tok[:, cols].astype(F32)
        tgrad[:, cols] = (grad * gain[:, cols] * inv[...] - values * coef[...]).astype(BF16)
        gst[0, :, cols] = jnp.sum(grad * values * inv[...], axis=0, keepdims=True) * scale
        return carry

    groups = nblk // grp
    cuts = [0, groups // 2, groups]

    def fwd_part(i):
        lax.fori_loop(cuts[i], cuts[i + 1], fwd_body, 0)

    def bwd_part(i):
        lax.fori_loop(cuts[i], cuts[i + 1], bwd_body, 0)

    def fwd_end():
        total = fwd[...]
        proj[...] = (total + bias[...]).astype(BF16)
        inner = jnp.sum(total * cot[...].astype(F32), axis=1, keepdims=True) / width
        coef[...] = inv[...] * inv[...] * inner

    def g_copy(n):
        dev = (partner, xdev, ydev)[n]
        return rdma(gst.at[n], grecv.at[n], g_s.at[n], g_r.at[n], dev)

    def g_step(n):
        g_copy(n).wait_recv()
        gst[n + 1] = gst[n] + grecv[n]
        if n < 2:
            g_copy(n + 1).start()

    def gz_copy(d):
        return rdma(gst.at[3], gz.at[z], gz_s.at[d - 1], gz_r.at[z], others[d - 1])

    def gz_got(d):
        q = (z + d) % planes
        return rdma(gst.at[3], gz.at[q], gz_s.at[d - 1], gz_r.at[q], others[d - 1])

    own_local.wait()
    fwd[...] = jnp.zeros_like(fwd)
    gst[0, :, width:] = jnp.sum(cot[...].astype(F32), axis=0, keepdims=True) * scale
    early = list(range(NJ // 2))
    late = list(range(NJ // 2, NJ))
    for j in early:
        core_sum(j)
        first_send(j)
    for j in late:
        core_sum(j)
    ag_arrive(1)
    for j in early:
        second_send(j)
    for j in late:
        first_send(j)
    for t in range(2, planes - 1):
        ag_side(t - 1)
        ag_arrive(t)
    for j in early:
        place(j)
        z_step(j, 0)
    for j in late:
        second_send(j)
    for j in early:
        z_step(j, 1)
    ag_side(planes - 2)
    ag_arrive(planes - 1)
    for j in late:
        place(j)
        z_step(j, 0)
    for t in range(2, planes - 1):
        for j in early:
            z_step(j, t)
    for j in early:
        z_end(j)
    for j in late:
        z_step(j, 1)
    ag_side(planes - 1)
    for t in range(1, planes):
        ag_finish(t)
    own_partner.wait_send()
    rdma(
        w, span(2 * z + oc, 0, cap), agp_s.at[0, z], agp_r.at[0, z], partner
    ).wait_recv()
    fwd_part(0)
    for t in range(2, planes - 1):
        for j in late:
            z_step(j, t)
    fwd_part(1)
    for j in late:
        z_end(j)
    fwd_end()
    bwd_part(0)
    bwd_part(1)
    g_copy(0).start()

    def f_got(j, n):
        ids = [quad * 2 + oc]
        for q in (xq, yq, dq):
            ids += [q * 2 + c, q * 2 + oc]
        sender = ids[n]
        return rdma(
            fin.at[j, pl.ds(0, cap)], frecv.at[sender, j],
            f_s.at[j, n], f_r.at[j, sender], plane[n],
        )

    for j in range(NJ):
        for n in range(7):
            f_got(j, n).wait_recv()

        def body(u, carry):
            for n in range(8):
                wgrad[pl.ds(pl.multiple_of(u * BLK + j * SUB, SUB), SUB), n * BLK:(n + 1) * BLK] = (
                    frecv[n, j, u].astype(F32)
                )
            return carry

        lax.fori_loop(0, cap, body, 0)
        if j < 3:
            g_step(j)
        if j == 2:
            gz[z] = gst[3]
            for d in range(1, planes):
                gz_copy(d).start()

    for d in range(1, planes):
        gz_got(d).wait_recv()
    total = gz[0]
    for q in range(1, planes):
        total = total + gz[q]
    vec[...] = total
    for d in range(1, planes):
        gz_copy(d).wait_send()
    for n in range(3):
        g_copy(n).wait_send()

    for j in range(NJ):
        for cp in first_hop(j):
            cp.wait_send()
        second_hop(j).wait_send()
        for cp in f_copies(j):
            cp.wait_send()
        for t in range(planes - 1):
            @pl.when(z < planes - 1 - t)
            def _():
                up_copy(j, planes - 1 - t).wait_send()

            @pl.when(z > t)
            def _():
                dn_copy(j, t).wait_send()

    @pl.when(has_up)
    def _():
        own_z(0, updev).wait_send()

    @pl.when(has_dn)
    def _():
        own_z(1, dndev).wait_send()


def communicate(tokens, norm_gain, cotangent, key_bias, block_of_slot, block_slot, key_weight, scale):
    shard_count = lax.axis_size("shard")
    planes = shard_count // 2
    rows, cols = key_weight.shape
    cap = rows // BLK
    tok_count, width = tokens.shape
    nblk = width // BLK
    group = cols // (2 * QUAD)
    dma = pltpu.SemaphoreType.DMA
    vm = pltpu.VMEM
    return pl.pallas_call(
        functools.partial(comm_kernel, planes, cap, nblk, scale),
        out_shape=(
            jax.ShapeDtypeStruct((tok_count, cols), BF16),
            jax.ShapeDtypeStruct((tok_count, width), BF16),
            jax.ShapeDtypeStruct((rows, cols), F32),
            jax.ShapeDtypeStruct((1, width + cols), F32),
        ),
        in_specs=[
            pl.BlockSpec(memory_space=vm),
            pl.BlockSpec(memory_space=vm),
            pl.BlockSpec(memory_space=vm),
            pl.BlockSpec(memory_space=vm),
            pl.BlockSpec(memory_space=pltpu.SMEM),
            pl.BlockSpec(memory_space=pltpu.SMEM),
            pl.BlockSpec(memory_space=vm),
        ],
        out_specs=(pl.BlockSpec(memory_space=vm),) * 4,
        scratch_shapes=[
            vm((shard_count * cap, BLK, cols), BF16),
            vm((tok_count, 1), F32),
            vm((tok_count, 1), F32),
            vm((tok_count, cols), F32),
            vm((4, 1, width + cols), F32),
            vm((3, 1, width + cols), F32),
            vm((planes, 1, width + cols), F32),
            vm((2, NJ, QUAD, nblk, SUB, group), BF16),
            vm((NJ, QUAD, nblk, SUB, group), BF16),
            vm((NJ, 2, nblk, SUB, group), BF16),
            vm((NJ, nblk, SUB, group), BF16),
            vm((NJ, planes, 2 * cap, SUB, group), BF16),
            vm((NJ, planes, 2 * cap, SUB, group), BF16),
            vm((NJ, planes, 2 * cap, SUB, group), BF16),
            vm((NJ, 2 * cap, SUB, group), BF16),
            vm((2 * QUAD, NJ, cap, SUB, group), BF16),
            dma(()),
            dma((2, planes)), dma((planes,)),
            dma((planes,)), dma((planes,)),
            dma((planes,)), dma((planes,)),
            dma((4, planes)), dma((4, planes)),
            dma((NJ, 2)), dma((NJ, 2)),
            dma((NJ, 2)), dma((NJ, 2)),
            dma((NJ,)), dma((NJ,)),
            dma((NJ, planes)), dma((NJ, planes)),
            dma((NJ, planes)), dma((NJ, planes)),
            dma((NJ, 7)), dma((NJ, 8)),
            dma((3,)), dma((3,)),
            dma((planes,)), dma((planes,)),
        ],
        compiler_params=pltpu.CompilerParams(
            collective_id=0, has_side_effects=True, vmem_limit_bytes=67043328
        ),
    )(
        tokens, norm_gain[None, :], cotangent, key_bias[None, :], block_of_slot, block_slot,
        key_weight.reshape(cap, BLK, cols),
    )


def local(tokens, norm_gain, key_bias, key_weight, cotangent, block_slot):
    row_count, width = tokens.shape
    shard_count = lax.axis_size("shard")
    replicas = lax.axis_size("rep")
    cap = key_weight.shape[0] // BLK
    slot_total = shard_count * cap
    block_count = width // BLK
    grad_scale = float(row_count * shard_count * replicas) ** (-0.5)
    match = block_slot[None, :] == jnp.arange(slot_total, dtype=jnp.int32)[:, None]
    numbers = jnp.arange(1, block_count + 1, dtype=jnp.int32)[None, :]
    block_of_slot = jnp.sum(jnp.where(match, numbers, 0), axis=1) - 1
    projected, token_grad, weight_grad, vec = communicate(
        tokens, norm_gain, cotangent, key_bias, block_of_slot, block_slot, key_weight, grad_scale
    )
    if replicas > QUAD:
        groups = [list(range(i, replicas, QUAD)) for i in range(QUAD)]
        weight_grad, vec = lax.psum((weight_grad, vec), "rep", axis_index_groups=groups)
    return (projected, token_grad, weight_grad, vec[0, :width], vec[0, width:])


def solution(mesh):
    return jax.shard_map(
        local,
        mesh=mesh,
        in_specs=(
            P(("shard", "rep"), None),
            P(),
            P(),
            P("shard", None),
            P(("shard", "rep"), None),
            P(),
        ),
        out_specs=(
            P(("shard", "rep"), None),
            P(("shard", "rep"), None),
            P("shard", None),
            P(),
            P(),
        ),
        check_vma=False,
    )
```

profile of v0, /device:TPU:0, one launch (start us, length us, event | category | flops | bytes accessed | tf_op | source)
XLA Modules:
  0.0 166.1 jit_solution(16269594352273806643)
XLA Ops:
  0.6 0.7 select_reduce_fusion
  1.4 0.5 broadcast_add_fusion.bos
  1.9 153.0 %shard_map.101 = (bf16[384,1024]{1,0:T(8,128)(2,1)}, bf16[384,5120]{1,0:T(8,128)(2,1)}, f32[1024,1024]{1,0:T(8,128)}, f32[1,6144]{1,0:T(1,128)}) custom-call(bf16[384,5120]{1,0:T(8,128)(2,1)} %tok.1, f32[1,5120]{1,0:T(1,128)} %bitcast.7, bf16[384,1024]{1,0:T(8,128)(2,1)} %cot.1, f32[1,1024]{1,0:T(1,128)} %bitcast.9, s32[64]{0:T(128)} %broadcast_add_fusion.bos, ...), custom_call_target="tpu_custom_call" | custom-call | tf_op jit(solution)/shard_map/pallas_call | solution.py:520
  154.9 1.3 slice.7
  156.2 1.3 slice.6
  157.5 2.1 %copy.14 = bf16[384,1024]{1,0:T(8,128)(2,1)} copy(bf16[384,1024]{1,0:T(8,128)(2,1)} %get-tuple-element.18) | data formatting | bytes 1572864
  159.6 0.0 copy-start
  159.6 4.4 %copy.15 = bf16[384,5120]{1,0:T(8,128)(2,1)} copy(bf16[384,5120]{1,0:T(8,128)(2,1)} %get-tuple-element.19) | data formatting | bytes 7864320
  164.0 0.0 copy-done
  164.0 2.0 %copy.16 = f32[1024,1024]{1,0:T(8,128)} copy(f32[1024,1024]{1,0:T(8,128)S(1)} %copy-done) | data formatting | bytes 8388608
  (1 shorter events, 0.0 us)
Async XLA Ops:
  159.6 4.4 %copy-start = (f32[1024,1024]{1,0:T(8,128)S(1)}, f32[1024,1024]{1,0:T(8,128)}, u32[]{:S(2)}) copy-start(f32[1024,1024]{1,0:T(8,128)} %get-tuple-element.20) | copy-start | bytes 12582916
where the time goes:
time: 166 us
  Pallas kernels  153 us (92%)
  local copies, waits for them, and re-layouts  11.1 us (7%)
    pallas_call x1, Pallas kernels, communicate(): pl.pallas_call(functools.partial(comm_kernel, planes, cap, nblk, scale),...  153 us
    unnamed x5, local copies, waits for them, and re-layouts  8.52 us

commit v1 on v0

v1 whole, which is shorter than its diff:
```python
import functools
import jax
import jax.numpy as jnp
from jax import lax
from jax.experimental import pallas as pl
from jax.experimental.pallas import tpu as pltpu
from jax.sharding import PartitionSpec as P

BLK = 128
EPS = 1e-06
NJ = 8
NI = 2
SUB = BLK // NJ
QUAD = 4
MESH = pl.DeviceIdType.MESH
F32 = jnp.float32
BF16 = jnp.bfloat16
COMPUTE = 2

OWN, OWNP, SQ, TERM, SUM, HOP1, HOP2, PLACE, ZUP, ZDN, ZEND, PASS = range(12)
FWD, BWD, AGZ, AGSIDE, AGPART, AGEND, G0, GSTEP, GEND = range(12, 21)
COMMON = (SQ, TERM, FWD, BWD)

TUNED = (
    (
        (OWN, 0, 0), (OWN, 1, 0), (OWN, 2, 0), (OWN, 3, 0), (OWNP, 0, 0), (SQ, 0, 0),
        (TERM, 0, 0), (TERM, 1, 0), (AGZ, 1, 0), (AGSIDE, 1, 0), (SUM, 0, 0), (HOP1, 0, 0),
        (SUM, 1, 0), (HOP1, 1, 0), (SUM, 2, 0), (HOP1, 2, 0), (SUM, 3, 0), (HOP1, 3, 0),
        (SUM, 4, 0), (SUM, 5, 0), (HOP1, 4, 0), (HOP1, 5, 0), (SUM, 6, 0), (SUM, 7, 0),
        (HOP1, 7, 0), (AGZ, 1, 1), (SUM, 0, 1), (SUM, 1, 1), (HOP1, 1, 1), (SUM, 2, 1),
        (SUM, 3, 1), (AGSIDE, 1, 1), (SUM, 4, 1), (SUM, 5, 1), (SUM, 6, 1), (HOP1, 3, 1),
        (SUM, 7, 1), (AGPART, 1, 0), (AGZ, 1, 2), (AGSIDE, 1, 2), (HOP2, 1, 0), (HOP1, 0, 1),
        (AGZ, 1, 3), (HOP2, 3, 0), (AGSIDE, 1, 3), (HOP1, 2, 1), (AGZ, 2, 0), (AGSIDE, 2, 0),
        (HOP2, 0, 0), (HOP2, 2, 0), (AGPART, 1, 1), (AGZ, 2, 1), (HOP2, 4, 0), (AGSIDE, 2, 1),
        (HOP1, 5, 1), (AGPART, 1, 2), (HOP2, 0, 1), (AGZ, 2, 2), (AGSIDE, 2, 2), (HOP2, 1, 1),
        (HOP2, 3, 1), (AGPART, 1, 3), (HOP2, 5, 0), (AGZ, 2, 3), (HOP1, 4, 1), (AGSIDE, 2, 3),
        (AGPART, 2, 0), (HOP2, 7, 0), (AGZ, 3, 0), (AGSIDE, 3, 0), (HOP2, 2, 1), (HOP1, 7, 1),
        (PLACE, 0, 0), (ZUP, 0, 3), (ZUP, 0, 2), (ZUP, 0, 1), (AGPART, 2, 1), (PLACE, 1, 0),
        (ZUP, 1, 3), (ZUP, 1, 2), (ZUP, 1, 1), (AGZ, 3, 1), (AGSIDE, 3, 1), (PLACE, 3, 0),
        (ZUP, 3, 3), (ZUP, 3, 2), (ZUP, 3, 1), (AGPART, 2, 2), (AGZ, 3, 2), (AGSIDE, 3, 2),
        (HOP2, 5, 1), (HOP2, 4, 1), (HOP1, 6, 0), (AGPART, 2, 3), (PLACE, 2, 0), (ZUP, 2, 3),
        (ZUP, 2, 2), (ZUP, 2, 1), (AGZ, 3, 3), (AGSIDE, 3, 3), (HOP1, 6, 1), (ZEND, 1, 0),
        (AGPART, 3, 0), (HOP2, 7, 1), (AGPART, 3, 1), (AGPART, 3, 2), (PLACE, 5, 0), (ZUP, 5, 3),
        (ZUP, 5, 2), (ZUP, 5, 1), (PLACE, 4, 0), (ZUP, 4, 3), (ZUP, 4, 2), (ZUP, 4, 1),
        (HOP2, 6, 0), (AGPART, 3, 3), (HOP2, 6, 1), (PASS, 1, 0), (AGEND, 0, 0), (FWD, 0, 0),
        (ZEND, 0, 0), (PLACE, 7, 0), (ZUP, 7, 3), (ZUP, 7, 2), (ZUP, 7, 1), (PLACE, 6, 0),
        (ZUP, 6, 3), (ZUP, 6, 2), (ZUP, 6, 1), (FWD, 1, 0), (PASS, 0, 0), (ZEND, 2, 0),
        (BWD, 0, 0), (ZEND, 3, 0), (PASS, 2, 0), (ZEND, 4, 0), (BWD, 1, 0), (PASS, 3, 0),
        (ZEND, 5, 0), (G0, 0, 0), (PASS, 4, 0), (GSTEP, 0, 0), (ZEND, 7, 0), (PASS, 5, 0),
        (GSTEP, 1, 0), (ZEND, 6, 0), (PASS, 7, 0), (GSTEP, 2, 0), (PASS, 6, 0), (GEND, 0, 0),
    ),
    (
        (OWN, 0, 0), (OWN, 1, 0), (OWN, 2, 0), (OWN, 3, 0), (OWNP, 0, 0), (SQ, 0, 0),
        (TERM, 0, 0), (TERM, 1, 0), (SUM, 0, 0), (SUM, 1, 0), (AGZ, 0, 0), (AGZ, 2, 0),
        (AGSIDE, 0, 0), (AGSIDE, 2, 0), (SUM, 2, 0), (SUM, 3, 0), (SUM, 4, 0), (SUM, 5, 0),
        (SUM, 6, 0), (HOP1, 0, 0), (HOP1, 1, 0), (HOP1, 3, 0), (HOP1, 5, 0), (SUM, 7, 0),
        (HOP1, 7, 0), (SUM, 0, 1), (SUM, 1, 1), (SUM, 2, 1), (HOP1, 0, 1), (HOP1, 1, 1),
        (SUM, 3, 1), (SUM, 4, 1), (AGZ, 0, 1), (AGZ, 2, 1), (SUM, 5, 1), (SUM, 6, 1),
        (SUM, 7, 1), (AGSIDE, 0, 1), (HOP1, 3, 1), (AGPART, 0, 0), (HOP1, 5, 1), (AGZ, 0, 2),
        (AGZ, 2, 2), (AGSIDE, 2, 1), (AGPART, 2, 0), (AGSIDE, 0, 2), (AGZ, 0, 3), (AGZ, 2, 3),
        (HOP1, 2, 0), (AGSIDE, 2, 2), (HOP1, 2, 1), (AGZ, 3, 0), (AGSIDE, 3, 0), (AGSIDE, 0, 3),
        (AGPART, 0, 1), (AGZ, 3, 1), (AGSIDE, 3, 1), (AGSIDE, 2, 3), (AGPART, 2, 1), (AGPART, 0, 2),
        (AGZ, 3, 2), (HOP2, 1, 0), (AGSIDE, 3, 2), (HOP2, 1, 1), (AGPART, 2, 2), (AGZ, 3, 3),
        (HOP1, 4, 0), (AGSIDE, 3, 3), (HOP1, 4, 1), (AGPART, 3, 0), (AGPART, 0, 3), (HOP2, 3, 0),
        (HOP2, 0, 0), (HOP2, 3, 1), (AGPART, 3, 1), (HOP2, 0, 1), (AGPART, 2, 3), (HOP1, 6, 0),
        (HOP2, 2, 0), (PLACE, 1, 0), (ZUP, 1, 3), (HOP2, 2, 1), (HOP1, 6, 1), (ZUP, 1, 2),
        (HOP1, 7, 1), (AGPART, 3, 2), (ZDN, 1, 0), (HOP2, 5, 0), (ZEND, 1, 0), (HOP2, 4, 0),
        (HOP2, 5, 1), (AGPART, 3, 3), (HOP2, 4, 1), (HOP2, 7, 0), (AGEND, 0, 0), (FWD, 0, 0),
        (FWD, 1, 0), (PLACE, 0, 0), (ZUP, 0, 3), (ZUP, 0, 2), (PLACE, 2, 0), (ZUP, 2, 3),
        (ZUP, 2, 2), (PLACE, 3, 0), (ZUP, 3, 3), (ZUP, 3, 2), (BWD, 0, 0), (PASS, 1, 0),
        (ZDN, 0, 0), (BWD, 1, 0), (ZDN, 2, 0), (G0, 0, 0), (PLACE, 4, 0), (ZDN, 3, 0),
        (ZUP, 4, 3), (ZUP, 4, 2), (PLACE, 5, 0), (ZUP, 5, 3), (ZUP, 5, 2), (ZEND, 0, 0),
        (ZEND, 2, 0), (GSTEP, 0, 0), (HOP2, 6, 0), (HOP2, 6, 1), (HOP2, 7, 1), (ZEND, 3, 0),
        (ZDN, 4, 0), (PASS, 0, 0), (ZEND, 4, 0), (PASS, 2, 0), (GSTEP, 1, 0), (ZDN, 5, 0),
        (ZEND, 5, 0), (PLACE, 7, 0), (ZUP, 7, 3), (ZUP, 7, 2), (PLACE, 6, 0), (ZUP, 6, 3),
        (ZUP, 6, 2), (PASS, 3, 0), (PASS, 4, 0), (ZDN, 7, 0), (ZEND, 7, 0), (ZDN, 6, 0),
        (GSTEP, 2, 0), (ZEND, 6, 0), (PASS, 5, 0), (PASS, 7, 0), (PASS, 6, 0), (GEND, 0, 0),
    ),
)


def mirror(order, planes):
    flip = {ZUP: ZDN, ZDN: ZUP}
    out = []
    for step, a, b in order:
        if step in (ZUP, ZDN):
            b = planes - 1 - b
        if step in (AGZ, AGSIDE, AGPART):
            a = planes - 1 - a
        out.append((flip.get(step, step), a, b))
    return out


def plain_order(z, planes, cap):
    half = cap // 2
    out = [(OWN, k, 0) for k in range(half)] + [(OWNP, 0, 0), (SQ, 0, 0)]
    out += [(TERM, i, 0) for i in range(NI)]
    for step in (SUM, HOP1, HOP2):
        out += [(step, j, i) for j in range(NJ) for i in range(NI)]
    out += [(PLACE, j, 0) for j in range(NJ)]
    for step in (AGZ, AGSIDE, AGPART):
        for t in range(1, planes):
            for q in (z - t, z + t):
                if 0 <= q < planes:
                    out += [(step, q, k) for k in range(half)]
    for t in range(planes - 1):
        for j in range(NJ):
            if z < planes - 1 - t:
                out.append((ZUP, j, planes - 1 - t))
            if z > t:
                out.append((ZDN, j, t))
    for step in (ZEND, PASS):
        out += [(step, j, 0) for j in range(NJ)]
    out.append((AGEND, 0, 0))
    for step in (FWD, BWD):
        out += [(step, g, 0) for g in range(COMPUTE)]
    out.append((G0, 0, 0))
    out += [(GSTEP, n, 0) for n in range(3)]
    out.append((GEND, 0, 0))
    return out


def order_of(z, planes, cap):
    if planes == 4 and cap == 8:
        return list(TUNED[z]) if z < 2 else mirror(TUNED[planes - 1 - z], planes)
    return plain_order(z, planes, cap)


def split(order):
    parts, common = [[]], []
    for tok in order:
        if tok[0] in COMMON:
            common.append(tok)
            parts.append([])
        else:
            parts[-1].append(tok)
    return parts, common


def comm_kernel(
    planes, cap, nblk, scale,
    tok_h, gain_h, cot_h, bias_h, w_h, slot_of,
    proj, tgrad, frecv, vec,
    whole, tok, cot, gain, bias, inv, coef, fwd, gst, grecv, gz,
    part, drecv, r1, r2, slots, zup, zdn, bos,
    in_sem, agz_s, agz_r, ags_s, ags_r, agp_s, agp_r, own_s, own_r,
    d_s, d_r, r1_s, r1_r, r2_s, r2_r, zu_s, zu_r, zd_s, zd_r,
    f_s, f_r, p_s, p_r, g_s, g_r, gz_s, gz_r,
):
    s = lax.axis_index("shard")
    r = lax.axis_index("rep")
    z = s // 2
    c = s % 2
    quad = r % QUAD
    base = r - quad
    y = quad // 2
    x = quad % 2
    xq = y * 2 + (1 - x)
    yq = (1 - y) * 2 + x
    dq = (1 - y) * 2 + (1 - x)
    oc = 1 - c
    partner = (2 * z + oc, r)
    xdev = (s, base + xq)
    ydev = (s, base + yq)
    updev = (s + 2, r)
    dndev = (s - 2, r)
    near = [partner] + [(2 * z + cc, base + q) for q in (xq, yq) for cc in (c, oc)]
    others = [(2 * ((z + d) % planes) + c, r) for d in range(1, planes)]

    bar = pltpu.get_barrier_semaphore()
    for dev in near + others:
        pl.semaphore_signal(bar, inc=1, device_id=dev, device_id_type=MESH)

    loads = [
        pltpu.make_async_copy(w_h, whole.at[pl.ds(s * cap, cap)], in_sem.at[0]),
        pltpu.make_async_copy(tok_h, tok, in_sem.at[1]),
        pltpu.make_async_copy(cot_h, cot, in_sem.at[2]),
        pltpu.make_async_copy(gain_h, gain, in_sem.at[3]),
        pltpu.make_async_copy(bias_h, bias, in_sem.at[4]),
    ]
    for cp in loads:
        cp.start()

    def owner(u, carry):
        found = jnp.int32(-1)
        for b in range(nblk):
            found = jnp.where(slot_of[b] == u, b, found)
        bos[u] = found
        return carry

    lax.fori_loop(0, 2 * planes * cap, owner, 0)
    loads[0].wait()
    pl.semaphore_wait(bar, len(near) + len(others))

    def rdma(src, dst, ss, rs, dev):
        return pltpu.make_async_remote_copy(
            src_ref=src, dst_ref=dst, send_sem=ss, recv_sem=rs, device_id=dev, device_id_type=MESH
        )

    half = cap // 2
    quar = cap // 4
    hh = (x + y) % 2
    tokens_here, width = tok.shape
    wide = 4 * BLK
    nb = nblk // NI
    per_plane = 2 * cap

    def held(q, core, which, k):
        start = hh * half if which == 0 else (1 - hh) * half
        return whole.at[pl.ds((2 * q + core) * cap + start + k, 1)]

    def ag_z(q, d, k):
        ref = held(q, c, 0, k)
        return rdma(ref, ref, agz_s.at[d, q, k], agz_r.at[q, k], updev if d == 0 else dndev)

    def ag_side(q, which, k):
        ref = held(q, c, which, k)
        return rdma(ref, ref, ags_s.at[q, k], ags_r.at[q, k], xdev if k < quar else ydev)

    def ag_part(q, core, which, k):
        ref = held(q, core, which, k)
        return rdma(ref, ref, agp_s.at[which, q, k], agp_r.at[which, q, k], partner)

    def own_part(core):
        ref = whole.at[pl.ds((2 * z + core) * cap, cap)]
        return rdma(ref, ref, own_s, own_r, partner)

    def onward(zz, q):
        out = []
        if q <= zz < planes - 1:
            out.append(0)
        if q >= zz > 0:
            out.append(1)
        return out

    def d_copy(j, i):
        blocks = pl.ds(i * nb, nb)
        return rdma(
            part.at[oc, j, :, blocks], drecv.at[j, :, blocks], d_s.at[j, i], d_r.at[j, i], partner
        )

    def first_hop(j, i, n):
        q, dev = (xq, xdev) if j % 2 == 0 else (yq, ydev)
        q = (q, dq)[n]
        blocks = pl.ds(i * nb, nb)
        return rdma(
            part.at[c, j, q, blocks], r1.at[j, n, blocks], r1_s.at[j, i, n], r1_r.at[j, i, n], dev
        )

    def second_hop(j, i):
        far, dev = (yq, ydev) if j % 2 == 0 else (xq, xdev)
        blocks = pl.ds(i * nb, nb)
        return rdma(
            part.at[c, j, far, blocks], r2.at[j, blocks], r2_s.at[j, i], r2_r.at[j, i], dev
        )

    def add_to(dst, src, start, count):
        step = next(n for n in (10, 8, 5, 4, 2, 1) if count % n == 0)

        def body(i, carry):
            sl = pl.ds(start + i * step, step)
            dst[sl] = (dst[sl].astype(F32) + src[sl].astype(F32)).astype(BF16)
            return carry

        lax.fori_loop(0, count // step, body, 0)

    def z_copy(j, q, up):
        if up:
            return rdma(slots.at[j, q], zup.at[j, q], zu_s.at[j, q], zu_r.at[j, q], updev)
        return rdma(slots.at[j, q], zdn.at[j, q], zd_s.at[j, q], zd_r.at[j, q], dndev)

    my_id = quad * 2 + c

    def f_copies(zz, j):
        out = []
        for n, dev in enumerate(near):
            cc = oc if n in (0, 2, 4) else c
            out.append(
                rdma(
                    slots.at[j, zz, pl.ds(cc * cap, cap)], frecv.at[j, my_id],
                    f_s.at[j, n], f_r.at[j, my_id], dev,
                )
            )
        return out

    def f_got(j, q, core):
        sender = q * 2 + core
        return rdma(
            slots.at[j, 0, pl.ds(0, cap)], frecv.at[j, sender], f_s.at[j, 0], f_r.at[j, sender], partner
        )

    def f_pass(j):
        q, dev = (xq, ydev) if j % 2 == 0 else (yq, xdev)
        pair = frecv.at[j, pl.ds(q * 2, 2)]
        return rdma(pair, pair, p_s.at[j], p_r.at[j], dev)

    def f_passed(j):
        pair = frecv.at[j, pl.ds(dq * 2, 2)]
        return rdma(pair, pair, p_s.at[j], p_r.at[j], ydev if j % 2 == 0 else xdev)

    def g_copy(n):
        dev = (partner, xdev, ydev)[n]
        return rdma(gst.at[n], grecv.at[n], g_s.at[n], g_r.at[n], dev)

    def gz_copy(d, q):
        return rdma(gst.at[3], gz.at[q], gz_s.at[d - 1], gz_r.at[q], others[d - 1])

    def squares(i, acc):
        v = tok[:, pl.ds(pl.multiple_of(i * 2 * BLK, 2 * BLK), 2 * BLK)].astype(F32)
        v = v * v
        return acc + v[:, :BLK] + v[:, BLK:]

    def term(i, carry):
        cols = pl.ds(pl.multiple_of(i * wide, wide), wide)
        normed = (tok[:, cols].astype(F32) * inv[...] * gain[:, cols]).astype(BF16)
        res = lax.dot_general(
            normed, cot[...], (((0,), (0,)), ((), ())), preferred_element_type=F32
        )
        res = (res * scale).astype(BF16)
        group = res.shape[1] // (2 * QUAD)
        for b in range(wide // BLK):
            for j in range(NJ):
                lo = b * BLK + j * SUB
                for k in range(QUAD):
                    for cc in range(2):
                        col = (k * 2 + cc) * group
                        part[cc, j, k, i * (wide // BLK) + b] = res[lo:lo + SUB, col:col + group]
        return carry

    grp = 4
    gw = grp * BLK
    groups = nblk // grp
    cuts = [groups * i // COMPUTE for i in range(COMPUTE + 1)]

    def weight_group(g):
        return jnp.concatenate([whole[slot_of[g * grp + i]] for i in range(grp)], axis=0)

    def fwd_body(g, carry):
        cols = pl.ds(pl.multiple_of(g * gw, gw), gw)
        normed = (tok[:, cols].astype(F32) * inv[...] * gain[:, cols]).astype(BF16)
        fwd[...] += jnp.dot(normed, weight_group(g), preferred_element_type=F32)
        return carry

    def bwd_body(g, carry):
        cols = pl.ds(pl.multiple_of(g * gw, gw), gw)
        grad = lax.dot_general(
            cot[...], weight_group(g), (((1,), (1,)), ((), ())), preferred_element_type=F32
        )
        values = tok[:, cols].astype(F32)
        tgrad[:, cols] = (grad * gain[:, cols] * inv[...] - values * coef[...]).astype(BF16)
        gst[0, :, cols] = jnp.sum(grad * values * inv[...], axis=0, keepdims=True) * scale
        return carry

    def shared_step(step, a):
        if step == SQ:
            loads[1].wait()
            acc = lax.fori_loop(
                0, width // (2 * BLK), squares, jnp.zeros((tokens_here, BLK), F32)
            )
            inv[...] = lax.rsqrt(jnp.sum(acc, axis=1, keepdims=True) / width + EPS)
            for cp in loads[2:]:
                cp.wait()
        elif step == TERM:
            count = width // wide
            lax.fori_loop(a * count // NI, (a + 1) * count // NI, term, 0)
            for j in range(NJ):
                d_copy(j, a).start()
        elif step == FWD:
            if a == 0:
                fwd[...] = jnp.zeros_like(fwd)
            lax.fori_loop(cuts[a], cuts[a + 1], fwd_body, 0)
        else:
            if a == 0:
                total = fwd[...]
                proj[...] = (total + bias[...]).astype(BF16)
                inner = jnp.sum(total * cot[...].astype(F32), axis=1, keepdims=True) / width
                coef[...] = inv[...] * inv[...] * inner
                gst[0, :, width:] = jnp.sum(cot[...].astype(F32), axis=0, keepdims=True) * scale
            lax.fori_loop(cuts[a], cuts[a + 1], bwd_body, 0)

    def own_step(zz, step, a, b):
        if step == OWN:
            for d in onward(zz, zz):
                ag_z(zz, d, a).start()
        elif step == OWNP:
            own_part(c).start()
        elif step == AGZ:
            ag_z(a, 0, b).wait_recv()
            for d in onward(zz, a):
                ag_z(a, d, b).start()
            ag_part(a, c, 0, b).start()
        elif step == AGSIDE:
            ag_side(a, 0, b).start()
        elif step == AGPART:
            ag_side(a, 1, b).wait_recv()
            ag_part(a, c, 1, b).start()
        elif step == AGEND:
            for q in range(planes):
                if q != zz:
                    for k in range(half):
                        ag_part(q, oc, 0, k).wait_recv()
                        ag_part(q, oc, 1, k).wait_recv()
            own_part(oc).wait_recv()
        elif step == SUM:
            d_copy(a, b).wait()
            for k in range(QUAD):
                add_to(part.at[c, a, k], drecv.at[a, k], b * nb, nb)
        elif step == HOP1:
            first_hop(a, b, 1).start()
            first_hop(a, b, 0).start()
        elif step == HOP2:
            far = yq if a % 2 == 0 else xq
            first_hop(a, b, 1).wait_recv()
            add_to(part.at[c, a, far], r1.at[a, 1], b * nb, nb)
            second_hop(a, b).start()
            first_hop(a, b, 0).wait_recv()
            add_to(part.at[c, a, quad], r1.at[a, 0], b * nb, nb)
        elif step == PLACE:
            for i in range(NI):
                second_hop(a, i).wait_recv()
            add_to(part.at[c, a, quad], r2.at[a], 0, nblk)

            def body(i, carry):
                for u in range(per_plane):
                    k = bos[i * per_plane + u]
                    val = part[c, a, quad, jnp.maximum(k, 0)]
                    slots[a, i, u] = jnp.where(k >= 0, val.astype(F32), 0.0).astype(BF16)
                return carry

            lax.fori_loop(0, planes, body, 0)
        elif step == ZUP:
            if zz > 0:
                z_copy(a, b, True).wait_recv()
                add_to(slots.at[a, b], zup.at[a, b], 0, per_plane)
            z_copy(a, b, True).start()
        elif step == ZDN:
            if zz < planes - 1:
                z_copy(a, b, False).wait_recv()
                add_to(slots.at[a, b], zdn.at[a, b], 0, per_plane)
            z_copy(a, b, False).start()
        elif step == ZEND:
            if zz > 0:
                z_copy(a, zz, True).wait_recv()
                add_to(slots.at[a, zz], zup.at[a, zz], 0, per_plane)
            if zz < planes - 1:
                z_copy(a, zz, False).wait_recv()
                add_to(slots.at[a, zz], zdn.at[a, zz], 0, per_plane)
            for cp in f_copies(zz, a):
                cp.start()
            frecv[a, my_id] = slots[a, zz, pl.ds(c * cap, cap)]
        elif step == PASS:
            q = xq if a % 2 == 0 else yq
            f_got(a, q, 0).wait_recv()
            f_got(a, q, 1).wait_recv()
            f_pass(a).start()
        elif step == G0:
            g_copy(0).start()
        elif step == GSTEP:
            g_copy(a).wait_recv()
            gst[a + 1] = gst[a] + grecv[a]
            if a < 2:
                g_copy(a + 1).start()
            else:
                gz[zz] = gst[3]
                for d in range(1, planes):
                    gz_copy(d, zz).start()
        elif step == GEND:
            for d in range(1, planes):
                gz_copy(d, (zz + d) % planes).wait_recv()
            total = gz[0]
            for q in range(1, planes):
                total = total + gz[q]
            vec[...] = total

    def finish(zz):
        for j in range(NJ):
            f_got(j, quad, oc).wait_recv()
            q = yq if j % 2 == 0 else xq
            f_got(j, q, 0).wait_recv()
            f_got(j, q, 1).wait_recv()
            f_passed(j).wait_recv()
        for q in range(planes):
            for k in range(half):
                for d in onward(zz, q):
                    ag_z(q, d, k).wait_send()
                if q != zz:
                    ag_side(q, 0, k).wait_send()
                    ag_part(q, c, 0, k).wait_send()
                    ag_part(q, c, 1, k).wait_send()
        own_part(c).wait_send()
        for j in range(NJ):
            for i in range(NI):
                first_hop(j, i, 0).wait_send()
                first_hop(j, i, 1).wait_send()
                second_hop(j, i).wait_send()
            for q in range(planes):
                if q > zz:
                    z_copy(j, q, True).wait_send()
                if q < zz:
                    z_copy(j, q, False).wait_send()
            for cp in f_copies(zz, j):
                cp.wait_send()
            f_pass(j).wait_send()
        for n in range(3):
            g_copy(n).wait_send()
        for d in range(1, planes):
            gz_copy(d, zz).wait_send()

    plans = [split(order_of(zz, planes, cap)) for zz in range(planes)]
    common = plans[0][1]
    for n in range(len(common) + 1):
        for zz in range(planes):
            assert plans[zz][1] == common
            todo = plans[zz][0][n]
            last = n == len(common)
            if todo or last:
                @pl.when(z == zz)
                def _():
                    for tk in todo:
                        own_step(zz, *tk)
                    if last:
                        finish(zz)

        if n < len(common):
            shared_step(*common[n][:2])


def write_kernel(proj, tgrad, frecv, vec, proj_h, tgrad_h, wgrad_h, gain_h, bias_h, buf, sem, wsem):
    width = gain_h.shape[1]
    cap = frecv.shape[2]
    copies = [
        pltpu.make_async_copy(tgrad, tgrad_h, sem.at[0]),
        pltpu.make_async_copy(proj, proj_h, sem.at[1]),
        pltpu.make_async_copy(vec.at[:, :width], gain_h, sem.at[2]),
        pltpu.make_async_copy(vec.at[:, width:], bias_h, sem.at[3]),
    ]
    for cp in copies:
        cp.start()
    for u in range(cap):
        for j in range(NJ):
            for n in range(2 * QUAD):
                buf[u, j * SUB:(j + 1) * SUB, n * BLK:(n + 1) * BLK] = frecv[j, n, u].astype(F32)
        cp = pltpu.make_async_copy(buf.at[u], wgrad_h.at[u], wsem.at[u])
        cp.start()
        copies.append(cp)
    for cp in copies:
        cp.wait()


def communicate(tokens, norm_gain, cotangent, key_bias, block_slot, key_weight, scale):
    shard_count = lax.axis_size("shard")
    planes = shard_count // 2
    rows, cols = key_weight.shape
    cap = rows // BLK
    half = cap // 2
    tok_count, width = tokens.shape
    nblk = width // BLK
    group = cols // (2 * QUAD)
    dma = pltpu.SemaphoreType.DMA
    vm = pltpu.VMEM
    hbm = pl.BlockSpec(memory_space=pl.ANY)
    local = pl.BlockSpec(memory_space=vm)
    held = pl.pallas_call(
        functools.partial(comm_kernel, planes, cap, nblk, scale),
        out_shape=(
            vm((tok_count, cols), BF16),
            vm((tok_count, width), BF16),
            vm((NJ, 2 * QUAD, cap, SUB, group), BF16),
            vm((1, width + cols), F32),
        ),
        in_specs=[hbm, hbm, hbm, hbm, hbm, pl.BlockSpec(memory_space=pltpu.SMEM)],
        out_specs=(local,) * 4,
        scratch_shapes=[
            vm((shard_count * cap, BLK, cols), BF16),
            vm((tok_count, width), BF16),
            vm((tok_count, cols), BF16),
            vm((1, width), F32),
            vm((1, cols), F32),
            vm((tok_count, 1), F32),
            vm((tok_count, 1), F32),
            vm((tok_count, cols), F32),
            vm((4, 1, width + cols), F32),
            vm((3, 1, width + cols), F32),
            vm((planes, 1, width + cols), F32),
            vm((2, NJ, QUAD, nblk, SUB, group), BF16),
            vm((NJ, QUAD, nblk, SUB, group), BF16),
            vm((NJ, 2, nblk, SUB, group), BF16),
            vm((NJ, nblk, SUB, group), BF16),
            vm((NJ, planes, 2 * cap, SUB, group), BF16),
            vm((NJ, planes, 2 * cap, SUB, group), BF16),
            vm((NJ, planes, 2 * cap, SUB, group), BF16),
            pltpu.SMEM((shard_count * cap,), jnp.int32),
            dma((5,)),
            dma((2, planes, half)), dma((planes, half)),
            dma((planes, half)), dma((planes, half)),
            dma((2, planes, half)), dma((2, planes, half)),
            dma(()), dma(()),
            dma((NJ, NI)), dma((NJ, NI)),
            dma((NJ, NI, 2)), dma((NJ, NI, 2)),
            dma((NJ, NI)), dma((NJ, NI)),
            dma((NJ, planes)), dma((NJ, planes)),
            dma((NJ, planes)), dma((NJ, planes)),
            dma((NJ, 5)), dma((NJ, 8)),
            dma((NJ,)), dma((NJ,)),
            dma((3,)), dma((3,)),
            dma((planes,)), dma((planes,)),
        ],
        compiler_params=pltpu.CompilerParams(
            collective_id=0, has_side_effects=True, vmem_limit_bytes=54 * 2**20
        ),
    )(
        tokens, norm_gain[None, :], cotangent, key_bias[None, :],
        key_weight.reshape(cap, BLK, cols), block_slot,
    )
    return pl.pallas_call(
        write_kernel,
        out_shape=(
            jax.ShapeDtypeStruct((tok_count, cols), BF16),
            jax.ShapeDtypeStruct((tok_count, width), BF16),
            jax.ShapeDtypeStruct((cap, BLK, cols), F32),
            jax.ShapeDtypeStruct((1, width), F32),
            jax.ShapeDtypeStruct((1, cols), F32),
        ),
        in_specs=[local] * 4,
        out_specs=(hbm,) * 5,
        scratch_shapes=[vm((cap, BLK, cols), F32), dma((4,)), dma((cap,))],
        compiler_params=pltpu.CompilerParams(vmem_limit_bytes=8 * 2**20),
    )(*held)


def local(tokens, norm_gain, key_bias, key_weight, cotangent, block_slot):
    row_count, width = tokens.shape
    shard_count = lax.axis_size("shard")
    replicas = lax.axis_size("rep")
    grad_scale = float(row_count * shard_count * replicas) ** (-0.5)
    projected, token_grad, weight_grad, gain_grad, bias_grad = communicate(
        tokens, norm_gain, cotangent, key_bias, block_slot, key_weight, grad_scale
    )
    weight_grad = weight_grad.reshape(key_weight.shape)
    if replicas > QUAD:
        groups = [list(range(i, replicas, QUAD)) for i in range(QUAD)]
        weight_grad, gain_grad, bias_grad = lax.psum(
            (weight_grad, gain_grad, bias_grad), "rep", axis_index_groups=groups
        )
    return (projected, token_grad, weight_grad, gain_grad[0], bias_grad[0])


def solution(mesh):
    return jax.shard_map(
        local,
        mesh=mesh,
        in_specs=(
            P(("shard", "rep"), None),
            P(),
            P(),
            P("shard", None),
            P(("shard", "rep"), None),
            P(),
        ),
        out_specs=(
            P(("shard", "rep"), None),
            P(("shard", "rep"), None),
            P("shard", None),
            P(),
            P(),
        ),
        check_vma=False,
    )
```

time: 166 us -> 131 us (0.79)
  Pallas kernels: 153 us -> 131 us
  local copies, waits for them, and re-layouts: 11.1 us -> 0 us
    pallas_call x1, Pallas kernels: 153 us -> 127 us  [communicate(): pl.pallas_call(functools.partial(comm_kernel, planes, cap, nblk, scale),...]
    unnamed x5 -> x0, local copies, waits for them, and re-layouts: 8.52 us -> none
    pallas_call x0 -> x1, Pallas kernels: none -> 3.6 us  [communicate(): pl.pallas_call(write_kernel, out_shape=(jax.ShapeDtypeStruct((tok_count,...]
    slice x2 -> x0, local copies, waits for them, and re-layouts: 2.61 us -> none  [local(): return (projected, token_grad, weight_grad, vec[0, :width], vec[0, width:])]
where the time goes in v1:
time: 131 us
  Pallas kernels  131 us (100%)
    pallas_call x1, Pallas kernels, communicate(): pl.pallas_call(functools.partial(comm_kernel, planes, cap, nblk, scale),...  127 us
    pallas_call x1, Pallas kernels, communicate(): pl.pallas_call(write_kernel, out_shape=(jax.ShapeDtypeStruct((tok_count,...  3.6 us

profile of v1, /device:TPU:0, one launch (start us, length us, event | category | flops | bytes accessed | tf_op | source)
XLA Modules:
  0.0 131.3 jit_solution(8907035379614320196)
XLA Ops:
  0.6 126.9 %shard_map.101 = (bf16[384,1024]{1,0:T(8,128)(2,1)S(1)}, bf16[384,5120]{1,0:T(8,128)(2,1)S(1)}, bf16[8,8,8,16,128]{4,3,2,1,0:T(8,128)(2,1)S(1)}, f32[1,6144]{1,0:T(1,128)S(1)}) custom-call(bf16[384,5120]{1,0:T(8,128)(2,1)} %tok_h.1, f32[1,5120]{1,0:T(1,128)} %bitcast.7, bf16[384,1024]{1,0:T(8,128)(2,1)} %cot_h.1, f32[1,1024]{1,0:T(1,128)} %bitcast.8, ...), custom_call_target="tpu_custom_call" | custom-call | tf_op jit(solution)/shard_map/pallas_call | solution.py:563
  127.6 3.6 %shard_map.102 = (bf16[384,1024]{1,0:T(8,128)(2,1)}, bf16[384,5120]{1,0:T(8,128)(2,1)}, f32[8,128,1024]{2,1,0:T(8,128)}, f32[1,5120]{1,0:T(1,128)}, f32[1,1024]{1,0:T(1,128)}) custom-call(bf16[384,1024]{1,0:T(8,128)(2,1)S(1)} %get-tuple-element.14.proj, bf16[384,5120]{1,0:T(8,128)(2,1)S(1)} %get-tuple-element.15.tgrad, ...), custom_call_target="tpu_custom_call" | custom-call | tf_op jit(solution)/shard_map/pallas_call | solution.py:615

commit v2 on v1

v2 whole, which is shorter than its diff:
```python
import functools
import jax
import jax.numpy as jnp
from jax import lax
from jax.experimental import pallas as pl
from jax.experimental.pallas import tpu as pltpu
from jax.sharding import PartitionSpec as P

BLK = 128
EPS = 1e-06
NJ = 8
NI = 4
SUB = BLK // NJ
QUAD = 4
MESH = pl.DeviceIdType.MESH
F32 = jnp.float32
BF16 = jnp.bfloat16
COMPUTE = 3
FGRP = 8
BGRP = 4

OWN, OWNP, SQ, TERM, SUM, HOP1, HOP2, PLACE, ZUP, ZDN, ZEND, PASS = range(12)
FWD, BWD, AGZ, AGSIDE, AGPART, AGEND, G0, GSTEP, GEND, OWNER = range(12, 22)
COMMON = (SQ, TERM, FWD, BWD)

TUNED = (
    (
        (OWN, 0, 0), (OWN, 1, 0), (OWN, 2, 0), (OWN, 3, 0), (OWNP, 0, 0), (SQ, 0, 0), (TERM, 0, 0),
        (TERM, 1, 0), (SUM, 0, 0), (HOP1, 0, 0), (SUM, 1, 0), (HOP1, 1, 0), (SUM, 3, 0), (SUM, 2, 0),
        (SUM, 5, 0), (HOP1, 5, 0), (HOP1, 3, 0), (HOP1, 2, 0), (TERM, 2, 0), (AGZ, 1, 0), (AGSIDE, 1, 0),
        (SUM, 4, 1), (SUM, 1, 1), (HOP2, 2, 0), (SUM, 1, 2), (HOP1, 1, 1), (SUM, 3, 1), (HOP1, 3, 1),
        (SUM, 4, 0), (SUM, 5, 1), (TERM, 3, 0), (HOP1, 4, 1), (SUM, 7, 2), (HOP1, 5, 1), (HOP1, 7, 2),
        (SUM, 0, 3), (SUM, 3, 2), (SUM, 0, 1), (HOP2, 0, 0), (SUM, 3, 3), (HOP1, 0, 3), (SUM, 2, 1),
        (SUM, 5, 3), (AGZ, 1, 1), (SUM, 0, 2), (SUM, 2, 2), (SUM, 4, 3), (HOP2, 5, 0), (SUM, 6, 1),
        (HOP2, 1, 0), (HOP1, 3, 3), (HOP1, 0, 1), (SUM, 1, 3), (SUM, 5, 2), (HOP1, 1, 3), (HOP1, 2, 1),
        (HOP1, 4, 0), (HOP1, 4, 3), (HOP1, 3, 2), (SUM, 2, 3), (HOP1, 0, 2), (HOP1, 5, 3), (HOP2, 2, 1),
        (SUM, 4, 2), (HOP2, 4, 0), (HOP1, 2, 2), (AGPART, 1, 0), (HOP2, 0, 1), (AGZ, 1, 2), (HOP1, 1, 2),
        (HOP2, 3, 1), (HOP2, 3, 0), (HOP1, 2, 3), (HOP2, 0, 3), (AGSIDE, 1, 2), (SUM, 6, 2), (HOP1, 4, 2),
        (AGSIDE, 1, 1), (HOP2, 3, 3), (SUM, 7, 3), (HOP2, 1, 1), (SUM, 6, 3), (HOP2, 1, 2), (HOP2, 4, 1),
        (HOP2, 1, 3), (OWNER, 0, 0), (SUM, 7, 0), (HOP2, 5, 3), (AGZ, 2, 0), (HOP2, 2, 3), (HOP2, 0, 2),
        (HOP2, 3, 2), (AGSIDE, 2, 0), (AGZ, 1, 3), (HOP2, 4, 3), (HOP2, 4, 2), (AGSIDE, 1, 3), (HOP2, 2, 2),
        (SUM, 7, 1), (SUM, 6, 0), (PLACE, 0, 0), (HOP1, 7, 3), (PLACE, 1, 0), (ZUP, 0, 2), (AGZ, 2, 1),
        (PLACE, 3, 0), (AGZ, 2, 2), (AGSIDE, 2, 1), (AGPART, 1, 3), (HOP1, 6, 0), (PLACE, 4, 0), (ZUP, 1, 2),
        (ZUP, 0, 3), (AGSIDE, 2, 2), (HOP1, 5, 2), (AGZ, 2, 3), (PLACE, 2, 0), (ZUP, 4, 1), (AGSIDE, 2, 3),
        (AGZ, 3, 0), (AGSIDE, 3, 0), (ZUP, 1, 3), (HOP2, 5, 2), (ZUP, 2, 2), (HOP1, 6, 3), (AGZ, 3, 2),
        (ZUP, 3, 3), (AGSIDE, 3, 2), (ZUP, 4, 3), (HOP1, 7, 1), (ZUP, 3, 1), (AGPART, 1, 1), (AGPART, 2, 0),
        (AGZ, 3, 1), (HOP2, 5, 1), (AGSIDE, 3, 1), (ZUP, 2, 3), (AGPART, 1, 2), (AGZ, 3, 3), (ZUP, 3, 2),
        (HOP1, 6, 1), (AGSIDE, 3, 3), (HOP1, 7, 0), (AGPART, 3, 2), (HOP2, 6, 3), (HOP2, 6, 0), (PLACE, 5, 0),
        (ZUP, 4, 2), (AGPART, 2, 2), (HOP1, 6, 2), (ZUP, 5, 1), (ZUP, 5, 3), (ZUP, 0, 1), (ZUP, 1, 1),
        (HOP2, 7, 3), (AGPART, 3, 0), (AGPART, 2, 3), (AGPART, 3, 1), (ZUP, 2, 1), (AGPART, 2, 1), (HOP2, 6, 1),
        (AGPART, 3, 3), (HOP2, 7, 1), (HOP2, 7, 2), (ZUP, 5, 2), (HOP2, 6, 2), (HOP2, 7, 0), (AGEND, 0, 0),
        (FWD, 0, 0), (ZEND, 1, 0), (FWD, 1, 0), (ZEND, 2, 0), (PLACE, 6, 0), (ZUP, 6, 3), (PLACE, 7, 0),
        (ZUP, 7, 3), (ZUP, 6, 2), (ZUP, 7, 1), (ZEND, 3, 0), (FWD, 2, 0), (ZUP, 7, 2), (PASS, 1, 0),
        (BWD, 0, 0), (PASS, 2, 0), (ZEND, 4, 0), (ZEND, 0, 0), (ZUP, 6, 1), (BWD, 1, 0), (ZEND, 5, 0),
        (BWD, 2, 0), (G0, 0, 0), (GSTEP, 0, 0), (ZEND, 6, 0), (PASS, 5, 0), (ZEND, 7, 0), (PASS, 4, 0),
        (PASS, 3, 0), (GSTEP, 1, 0), (PASS, 6, 0), (PASS, 0, 0), (PASS, 7, 0), (GEND, 0, 0),
    ),
    (
        (OWN, 0, 0), (OWN, 1, 0), (OWN, 2, 0), (OWN, 3, 0), (OWNP, 0, 0), (SQ, 0, 0), (TERM, 0, 0),
        (TERM, 1, 0), (SUM, 0, 0), (SUM, 3, 0), (SUM, 2, 0), (HOP1, 2, 0), (SUM, 1, 0), (HOP1, 3, 0),
        (HOP1, 1, 0), (HOP1, 0, 0), (TERM, 2, 0), (SUM, 1, 1), (HOP1, 1, 1), (SUM, 0, 1), (SUM, 3, 1),
        (AGZ, 2, 0), (SUM, 4, 1), (AGSIDE, 2, 0), (HOP2, 0, 0), (SUM, 7, 1), (SUM, 3, 2), (SUM, 1, 2),
        (HOP1, 4, 1), (HOP1, 1, 2), (AGZ, 0, 0), (HOP1, 7, 1), (SUM, 6, 1), (AGSIDE, 0, 0), (SUM, 5, 2),
        (AGZ, 2, 1), (HOP1, 3, 1), (HOP2, 4, 1), (HOP1, 3, 2), (SUM, 0, 2), (AGZ, 2, 2), (AGSIDE, 2, 2),
        (TERM, 3, 0), (AGSIDE, 2, 1), (AGZ, 2, 3), (SUM, 0, 3), (HOP1, 0, 3), (HOP2, 1, 0), (AGZ, 0, 1),
        (HOP1, 0, 2), (SUM, 1, 3), (HOP1, 1, 3), (AGZ, 0, 2), (AGSIDE, 0, 2), (AGZ, 0, 3), (AGSIDE, 0, 1),
        (SUM, 2, 1), (AGSIDE, 0, 3), (HOP2, 3, 2), (SUM, 7, 0), (SUM, 7, 3), (HOP2, 1, 3), (AGPART, 2, 1),
        (HOP2, 1, 1), (SUM, 6, 0), (HOP1, 0, 1), (SUM, 4, 0), (AGZ, 3, 0), (HOP1, 7, 3), (SUM, 2, 3),
        (SUM, 6, 2), (SUM, 5, 0), (SUM, 5, 3), (HOP2, 0, 2), (HOP1, 6, 2), (HOP2, 0, 3), (SUM, 2, 2),
        (AGSIDE, 2, 3), (SUM, 7, 2), (AGZ, 3, 2), (AGPART, 0, 2), (SUM, 3, 3), (HOP2, 3, 1), (HOP2, 0, 1),
        (AGZ, 3, 1), (AGSIDE, 3, 0), (AGSIDE, 3, 1), (AGSIDE, 3, 2), (AGZ, 3, 3), (HOP2, 1, 2), (HOP1, 2, 2),
        (AGSIDE, 3, 3), (AGPART, 2, 0), (OWNER, 0, 0), (AGPART, 3, 2), (AGPART, 3, 0), (HOP2, 3, 0), (AGPART, 3, 1),
        (AGPART, 0, 1), (HOP1, 2, 3), (AGPART, 0, 0), (SUM, 4, 2), (AGPART, 0, 3), (PLACE, 1, 0), (HOP2, 2, 0),
        (HOP1, 2, 1), (ZUP, 1, 3), (HOP1, 3, 3), (SUM, 5, 1), (SUM, 4, 3), (AGPART, 3, 3), (HOP1, 4, 2),
        (PLACE, 0, 0), (HOP1, 5, 0), (AGPART, 2, 3), (HOP2, 2, 3), (HOP2, 2, 2), (HOP2, 7, 3), (HOP2, 3, 3),
        (HOP2, 2, 1), (HOP1, 5, 2), (HOP1, 4, 0), (ZUP, 0, 2), (SUM, 6, 3), (ZUP, 0, 3), (HOP1, 5, 3),
        (HOP1, 5, 1), (AGPART, 2, 2), (HOP1, 4, 3), (AGEND, 0, 0), (FWD, 0, 0), (HOP2, 4, 0), (HOP1, 6, 1),
        (ZUP, 1, 2), (PLACE, 3, 0), (ZUP, 3, 3), (HOP1, 6, 3), (HOP2, 4, 2), (FWD, 1, 0), (ZDN, 1, 0),
        (HOP2, 4, 3), (HOP2, 5, 0), (ZUP, 3, 2), (ZDN, 0, 0), (PLACE, 2, 0), (ZUP, 2, 3), (FWD, 2, 0),
        (HOP1, 7, 2), (HOP1, 7, 0), (HOP2, 5, 1), (HOP2, 6, 1), (HOP2, 6, 2), (HOP2, 5, 3), (ZDN, 3, 0),
        (HOP2, 5, 2), (BWD, 0, 0), (HOP2, 7, 1), (HOP2, 6, 3), (PLACE, 4, 0), (ZDN, 2, 0), (ZEND, 0, 0),
        (ZUP, 4, 3), (PLACE, 5, 0), (HOP1, 6, 0), (ZEND, 1, 0), (ZUP, 4, 2), (ZUP, 5, 3), (ZDN, 4, 0),
        (ZUP, 2, 2), (BWD, 1, 0), (HOP2, 7, 0), (ZUP, 5, 2), (HOP2, 7, 2), (HOP2, 6, 0), (ZEND, 3, 0),
        (ZDN, 5, 0), (ZEND, 4, 0), (BWD, 2, 0), (G0, 0, 0), (PLACE, 6, 0), (ZUP, 6, 3), (PASS, 1, 0),
        (PLACE, 7, 0), (ZEND, 5, 0), (ZUP, 7, 3), (ZUP, 6, 2), (PASS, 0, 0), (ZDN, 6, 0), (ZEND, 2, 0),
        (GSTEP, 0, 0), (PASS, 4, 0), (PASS, 3, 0), (ZUP, 7, 2), (ZDN, 7, 0), (ZEND, 6, 0), (PASS, 5, 0),
        (ZEND, 7, 0), (GSTEP, 1, 0), (PASS, 6, 0), (PASS, 7, 0), (PASS, 2, 0), (GEND, 0, 0),
    ),
)


def mirror(order, planes):
    flip = {ZUP: ZDN, ZDN: ZUP}
    out = []
    for step, a, b in order:
        if step in (ZUP, ZDN):
            b = planes - 1 - b
        if step in (AGZ, AGSIDE, AGPART):
            a = planes - 1 - a
        out.append((flip.get(step, step), a, b))
    return out


def plain_order(z, planes, cap):
    half = cap // 2
    out = [(OWN, k, 0) for k in range(half)] + [(OWNP, 0, 0), (SQ, 0, 0), (OWNER, 0, 0)]
    out += [(TERM, i, 0) for i in range(NI)]
    for step in (SUM, HOP1, HOP2):
        out += [(step, j, i) for j in range(NJ) for i in range(NI)]
    out += [(PLACE, j, 0) for j in range(NJ)]
    for step in (AGZ, AGSIDE, AGPART):
        for t in range(1, planes):
            for q in (z - t, z + t):
                if 0 <= q < planes:
                    out += [(step, q, k) for k in range(half)]
    for t in range(planes - 1):
        for j in range(NJ):
            if z < planes - 1 - t:
                out.append((ZUP, j, planes - 1 - t))
            if z > t:
                out.append((ZDN, j, t))
    for step in (ZEND, PASS):
        out += [(step, j, 0) for j in range(NJ)]
    out.append((AGEND, 0, 0))
    for step in (FWD, BWD):
        out += [(step, g, 0) for g in range(COMPUTE)]
    out.append((G0, 0, 0))
    out += [(GSTEP, n, 0) for n in range(2)]
    out.append((GEND, 0, 0))
    return out


def order_of(z, planes, cap):
    if planes == 4 and cap == 8:
        return list(TUNED[z]) if z < 2 else mirror(TUNED[planes - 1 - z], planes)
    return plain_order(z, planes, cap)


def split(order):
    parts, common = [[]], []
    for tok in order:
        if tok[0] in COMMON:
            common.append(tok)
            parts.append([])
        else:
            parts[-1].append(tok)
    return parts, common


def comm_kernel(
    planes, cap, nblk, scale,
    tok_h, gain_h, cot_h, bias_h, w_h, slot_of,
    proj, tgrad, frecv, vec,
    whole, tok, cot, gain, bias, inv, coef, fwd, gst, grecv, gz,
    part, drecv, r1, r2, slots, zup, zdn, bos,
    in_sem, agz_r, ags_r, agp_r, d_r, r1_r, r2_r, z_r, pass_r, end_r, g_r, gz_r, sent,
):
    s = lax.axis_index("shard")
    r = lax.axis_index("rep")
    z = s // 2
    c = s % 2
    quad = r % QUAD
    base = r - quad
    y = quad // 2
    x = quad % 2
    xq = y * 2 + (1 - x)
    yq = (1 - y) * 2 + x
    dq = (1 - y) * 2 + (1 - x)
    oc = 1 - c
    partner = (2 * z + oc, r)
    xdev = (s, base + xq)
    ydev = (s, base + yq)
    updev = (s + 2, r)
    dndev = (s - 2, r)
    ddev = (s, base + dq)
    near = [partner] + [(2 * z + cc, base + q) for q in (xq, yq) for cc in (c, oc)]
    others = [(2 * ((z + d) % planes) + c, r) for d in range(1, planes)]

    bar = pltpu.get_barrier_semaphore()
    greet = near + [ddev] + others
    for dev in greet:
        pl.semaphore_signal(bar, inc=1, device_id=dev, device_id_type=MESH)

    loads = [
        pltpu.make_async_copy(w_h, whole.at[pl.ds(s * cap, cap)], in_sem.at[0]),
        pltpu.make_async_copy(tok_h, tok, in_sem.at[1]),
        pltpu.make_async_copy(cot_h, cot, in_sem.at[2]),
        pltpu.make_async_copy(gain_h, gain, in_sem.at[3]),
        pltpu.make_async_copy(bias_h, bias, in_sem.at[4]),
    ]
    for cp in loads:
        cp.start()

    def owner(u, carry):
        found = jnp.int32(-1)
        for b in range(nblk):
            found = jnp.where(slot_of[b] == u, b, found)
        bos[u] = found
        return carry

    loads[0].wait()
    pl.semaphore_wait(bar, len(greet))

    def rdma(src, dst, ss, rs, dev):
        return pltpu.make_async_remote_copy(
            src_ref=src, dst_ref=dst, send_sem=ss, recv_sem=rs, device_id=dev, device_id_type=MESH
        )

    half = cap // 2
    quar = cap // 4
    hh = (x + y) % 2
    tokens_here, width = tok.shape
    wide = 5 * BLK
    nb = nblk // NI
    per_plane = 2 * cap

    def held(q, core, which, k):
        start = hh * half if which == 0 else (1 - hh) * half
        return whole.at[pl.ds((2 * q + core) * cap + start + k, 1)]

    def ag_z(q, d, k):
        ref = held(q, c, 0, k)
        return rdma(ref, ref, sent.at[0], agz_r.at[q, k], updev if d == 0 else dndev)

    def ag_side(q, which, k):
        ref = held(q, c, which, k)
        return rdma(ref, ref, sent.at[1], ags_r.at[q, k], xdev if k < quar else ydev)

    def ag_part(q, which, k):
        ref = held(q, c, which, k)
        return rdma(ref, ref, sent.at[2], agp_r, partner)

    def own_part():
        ref = whole.at[pl.ds(s * cap, cap)]
        return rdma(ref, ref, sent.at[2], agp_r, partner)

    def slots_of(count, ss, rs):
        ref = whole.at[pl.ds(0, count)]
        return rdma(ref, ref, ss, rs, partner)

    def onward(zz, q):
        out = []
        if q <= zz < planes - 1:
            out.append(0)
        if q >= zz > 0:
            out.append(1)
        return out

    def d_copy(j, i):
        blocks = pl.ds(i * nb, nb)
        return rdma(
            part.at[oc, j, :, blocks], drecv.at[j, :, blocks], sent.at[3], d_r.at[j, i], partner
        )

    def first_hop(j, i, n):
        q, dev = (xq, xdev) if j % 2 == 0 else (yq, ydev)
        q = (q, dq)[n]
        blocks = pl.ds(i * nb, nb)
        return rdma(
            part.at[c, j, q, blocks], r1.at[j, n, blocks], sent.at[4], r1_r.at[j, i, n], dev
        )

    def second_hop(j, i):
        far, dev = (yq, ydev) if j % 2 == 0 else (xq, xdev)
        blocks = pl.ds(i * nb, nb)
        return rdma(
            part.at[c, j, far, blocks], r2.at[j, blocks], sent.at[5], r2_r.at[j], dev
        )

    def add_to(dst, src, start, count):
        step = next(n for n in (10, 8, 5, 4, 2, 1) if count % n == 0)

        def body(i, carry):
            sl = pl.ds(start + i * step, step)
            dst[sl] = (dst[sl].astype(F32) + src[sl].astype(F32)).astype(BF16)
            return carry

        lax.fori_loop(0, count // step, body, 0)

    def second_got(j):
        ref = r2.at[j]
        return rdma(ref, ref, sent.at[5], r2_r.at[j], partner)

    def z_copy(j, q, up, here):
        if up:
            return rdma(slots.at[j, q], zup.at[j, q], sent.at[6], z_r.at[j, q], updev)
        k = planes if q == here else q
        return rdma(slots.at[j, q], zdn.at[j, q], sent.at[7], z_r.at[j, k], dndev)

    my_id = quad * 2 + c

    def f_copies(zz, j):
        out = []
        for n, dev in enumerate(near):
            cc = oc if n in (0, 2, 4) else c
            onward_there = n in ((1, 2) if j % 2 == 0 else (3, 4))
            out.append(
                rdma(
                    slots.at[j, zz, pl.ds(cc * cap, cap)], frecv.at[j, my_id],
                    sent.at[8], pass_r.at[j] if onward_there else end_r, dev,
                )
            )
        return out

    def f_pass(j):
        q, dev = (xq, ydev) if j % 2 == 0 else (yq, xdev)
        pair = frecv.at[j, pl.ds(q * 2, 2)]
        return rdma(pair, pair, sent.at[8], end_r, dev)

    def f_pair(j):
        pair = frecv.at[j, pl.ds(0, 2)]
        return rdma(pair, pair, sent.at[8], pass_r.at[j], partner)

    def f_all(ss, rs, count):
        ref = frecv.at[:, pl.ds(0, count)]
        return rdma(ref, ref, ss, rs, partner)

    def g_copy(n):
        dev = (partner, xdev, ydev, ddev)[n]
        return rdma(gst.at[min(n, 1)], grecv.at[n], sent.at[9], g_r.at[n], dev)

    def gz_copy(d, q):
        return rdma(gst.at[2], gz.at[q], sent.at[9], gz_r, others[d - 1])

    def g_all(ref, ss, rs):
        return rdma(ref, ref, ss, rs, partner)

    def squares(i, acc):
        v = tok[:, pl.ds(pl.multiple_of(i * 2 * BLK, 2 * BLK), 2 * BLK)].astype(F32)
        v = v * v
        return acc + v[:, :BLK] + v[:, BLK:]

    def term(i, carry):
        cols = pl.ds(pl.multiple_of(i * wide, wide), wide)
        normed = (tok[:, cols].astype(F32) * inv[...] * gain[:, cols]).astype(BF16)
        res = lax.dot_general(
            normed, cot[...], (((0,), (0,)), ((), ())), preferred_element_type=F32
        )
        res = (res * scale).astype(BF16)
        group = res.shape[1] // (2 * QUAD)
        tgrad[:, cols] = normed
        for b in range(wide // BLK):
            for j in range(NJ):
                lo = b * BLK + j * SUB
                for k in range(QUAD):
                    for cc in range(2):
                        col = (k * 2 + cc) * group
                        part[cc, j, k, i * (wide // BLK) + b] = res[lo:lo + SUB, col:col + group]
        return carry

    def weight_group(g, grp):
        return jnp.concatenate([whole[slot_of[g * grp + i]] for i in range(grp)], axis=0)

    def cuts(grp, a):
        groups = nblk // grp
        return groups * a // COMPUTE, groups * (a + 1) // COMPUTE

    def fwd_body(g, carry):
        gw = FGRP * BLK
        cols = pl.ds(pl.multiple_of(g * gw, gw), gw)
        fwd[...] += jnp.dot(tgrad[:, cols], weight_group(g, FGRP), preferred_element_type=F32)
        return carry

    def bwd_body(g, carry):
        gw = BGRP * BLK
        cols = pl.ds(pl.multiple_of(g * gw, gw), gw)
        grad = lax.dot_general(
            cot[...], weight_group(g, BGRP), (((1,), (1,)), ((), ())), preferred_element_type=F32
        )
        values = tok[:, cols].astype(F32)
        grad = grad * inv[...]
        tgrad[:, cols] = (grad * gain[:, cols] - values * coef[...]).astype(BF16)
        gst[0, :, cols] = jnp.sum(grad * values, axis=0, keepdims=True) * scale
        return carry

    def shared_step(step, a):
        if step == SQ:
            loads[1].wait()
            acc = lax.fori_loop(
                0, width // (2 * BLK), squares, jnp.zeros((tokens_here, BLK), F32)
            )
            inv[...] = lax.rsqrt(jnp.sum(acc, axis=1, keepdims=True) / width + EPS)
            for cp in loads[2:]:
                cp.wait()
        elif step == TERM:
            count = width // wide
            lax.fori_loop(a * count // NI, (a + 1) * count // NI, term, 0)
            for j in range(NJ):
                d_copy(j, a).start()
        elif step == FWD:
            if a == 0:
                fwd[...] = jnp.zeros_like(fwd)
            lax.fori_loop(*cuts(FGRP, a), fwd_body, 0)
        else:
            if a == 0:
                total = fwd[...]
                proj[...] = (total + bias[...]).astype(BF16)
                inner = jnp.sum(total * cot[...].astype(F32), axis=1, keepdims=True) / width
                coef[...] = inv[...] * inv[...] * inner
                gst[0, :, width:] = jnp.sum(cot[...].astype(F32), axis=0, keepdims=True) * scale
            lax.fori_loop(*cuts(BGRP, a), bwd_body, 0)

    def own_step(zz, step, a, b):
        if step == OWN:
            for d in onward(zz, zz):
                ag_z(zz, d, a).start()
        elif step == OWNP:
            own_part().start()
        elif step == OWNER:
            lax.fori_loop(0, 2 * planes * cap, owner, 0)
        elif step == AGZ:
            ag_z(a, 0, b).wait_recv()
            for d in onward(zz, a):
                ag_z(a, d, b).start()
            ag_part(a, 0, b).start()
        elif step == AGSIDE:
            ag_side(a, 0, b).start()
        elif step == AGPART:
            ag_side(a, 1, b).wait_recv()
            ag_part(a, 1, b).start()
        elif step == AGEND:
            slots_of(planes * cap, sent.at[2], agp_r).wait_recv()
        elif step == SUM:
            d_copy(a, b).wait_recv()
            for k in range(QUAD):
                add_to(part.at[c, a, k], drecv.at[a, k], b * nb, nb)
        elif step == HOP1:
            first_hop(a, b, 1).start()
            first_hop(a, b, 0).start()
        elif step == HOP2:
            far = yq if a % 2 == 0 else xq
            first_hop(a, b, 1).wait_recv()
            add_to(part.at[c, a, far], r1.at[a, 1], b * nb, nb)
            second_hop(a, b).start()
            first_hop(a, b, 0).wait_recv()
            add_to(part.at[c, a, quad], r1.at[a, 0], b * nb, nb)
        elif step == PLACE:
            second_got(a).wait_recv()
            add_to(part.at[c, a, quad], r2.at[a], 0, nblk)

            def body(i, carry):
                for u in range(per_plane):
                    k = bos[i * per_plane + u]
                    val = part[c, a, quad, jnp.maximum(k, 0)]
                    slots[a, i, u] = jnp.where(k >= 0, val.astype(F32), 0.0).astype(BF16)
                return carry

            lax.fori_loop(0, planes, body, 0)
        elif step == ZUP:
            if zz > 0:
                z_copy(a, b, True, zz).wait_recv()
                add_to(slots.at[a, b], zup.at[a, b], 0, per_plane)
            z_copy(a, b, True, zz).start()
        elif step == ZDN:
            if zz < planes - 1:
                z_copy(a, b, False, zz).wait_recv()
                add_to(slots.at[a, b], zdn.at[a, b], 0, per_plane)
            z_copy(a, b, False, zz - 1).start()
        elif step == ZEND:
            if zz > 0:
                z_copy(a, zz, True, zz).wait_recv()
                add_to(slots.at[a, zz], zup.at[a, zz], 0, per_plane)
            if zz < planes - 1:
                z_copy(a, zz, False, zz).wait_recv()
                add_to(slots.at[a, zz], zdn.at[a, zz], 0, per_plane)
            for cp in f_copies(zz, a):
                cp.start()
            frecv[a, my_id] = slots[a, zz, pl.ds(c * cap, cap)]
        elif step == PASS:
            f_pair(a).wait_recv()
            f_pass(a).start()
        elif step == G0:
            g_copy(0).start()
        elif step == GSTEP:
            if a == 0:
                g_copy(0).wait_recv()
                gst[1] = gst[0] + grecv[0]
                for n in (3, 1, 2):
                    g_copy(n).start()
            else:
                for n in (1, 2, 3):
                    g_copy(n).wait_recv()
                gst[2] = (gst[1] + grecv[1]) + (grecv[2] + grecv[3])
                gz[zz] = gst[2]
                for d in range(1, planes):
                    gz_copy(d, zz).start()
        elif step == GEND:
            g_all(gz.at[pl.ds(0, planes - 1)], sent.at[9], gz_r).wait_recv()
            total = gz[0]
            for q in range(1, planes):
                total = total + gz[q]
            vec[...] = total

    def finish(zz):
        f_all(sent.at[8], end_r, 5).wait_recv()
        count = sum(len(onward(zz, q)) for q in range(planes)) * half
        slots_of(count, sent.at[0], agp_r).wait_send()
        slots_of((planes - 1) * half, sent.at[1], agp_r).wait_send()
        slots_of(planes * cap, sent.at[2], agp_r).wait_send()
        rdma(drecv, drecv, sent.at[3], end_r, partner).wait_send()
        rdma(r1, r1, sent.at[4], end_r, partner).wait_send()
        rdma(r2, r2, sent.at[5], end_r, partner).wait_send()
        for n, count in ((6, planes - 1 - zz), (7, zz)):
            if count:
                ref = slots.at[:, pl.ds(0, count)]
                rdma(ref, ref, sent.at[n], end_r, partner).wait_send()
        f_all(sent.at[8], end_r, 7).wait_send()
        g_all(gz.at[pl.ds(0, planes - 1)], sent.at[9], gz_r).wait_send()
        g_all(grecv, sent.at[9], gz_r).wait_send()

    plans = [split(order_of(zz, planes, cap)) for zz in range(planes)]
    common = plans[0][1]
    for n in range(len(common) + 1):
        for zz in range(planes):
            assert plans[zz][1] == common
            todo = plans[zz][0][n]
            last = n == len(common)
            if todo or last:
                @pl.when(z == zz)
                def _():
                    for tk in todo:
                        own_step(zz, *tk)
                    if last:
                        finish(zz)

        if n < len(common):
            shared_step(*common[n][:2])


def write_kernel(proj, tgrad, frecv, vec, proj_h, tgrad_h, wgrad_h, gain_h, bias_h, buf, sem, wsem):
    width = gain_h.shape[1]
    cap = frecv.shape[2]
    copies = [
        pltpu.make_async_copy(tgrad, tgrad_h, sem.at[0]),
        pltpu.make_async_copy(proj, proj_h, sem.at[1]),
        pltpu.make_async_copy(vec.at[:, :width], gain_h, sem.at[2]),
        pltpu.make_async_copy(vec.at[:, width:], bias_h, sem.at[3]),
    ]
    for cp in copies:
        cp.start()
    for u in range(cap):
        for j in range(NJ):
            for n in range(2 * QUAD):
                buf[u, j * SUB:(j + 1) * SUB, n * BLK:(n + 1) * BLK] = frecv[j, n, u].astype(F32)
        cp = pltpu.make_async_copy(buf.at[u], wgrad_h.at[u], wsem.at[u])
        cp.start()
        copies.append(cp)
    for cp in copies:
        cp.wait()


def communicate(tokens, norm_gain, cotangent, key_bias, block_slot, key_weight, scale):
    shard_count = lax.axis_size("shard")
    planes = shard_count // 2
    rows, cols = key_weight.shape
    cap = rows // BLK
    half = cap // 2
    tok_count, width = tokens.shape
    nblk = width // BLK
    group = cols // (2 * QUAD)
    dma = pltpu.SemaphoreType.DMA
    vm = pltpu.VMEM
    hbm = pl.BlockSpec(memory_space=pl.ANY)
    local = pl.BlockSpec(memory_space=vm)
    held = pl.pallas_call(
        functools.partial(comm_kernel, planes, cap, nblk, scale),
        out_shape=(
            vm((tok_count, cols), BF16),
            vm((tok_count, width), BF16),
            vm((NJ, 2 * QUAD, cap, SUB, group), BF16),
            vm((1, width + cols), F32),
        ),
        in_specs=[hbm, hbm, hbm, hbm, hbm, pl.BlockSpec(memory_space=pltpu.SMEM)],
        out_specs=(local,) * 4,
        scratch_shapes=[
            vm((shard_count * cap, BLK, cols), BF16),
            vm((tok_count, width), BF16),
            vm((tok_count, cols), BF16),
            vm((1, width), F32),
            vm((1, cols), F32),
            vm((tok_count, 1), F32),
            vm((tok_count, 1), F32),
            vm((tok_count, cols), F32),
            vm((3, 1, width + cols), F32),
            vm((4, 1, width + cols), F32),
            vm((planes, 1, width + cols), F32),
            vm((2, NJ, QUAD, nblk, SUB, group), BF16),
            vm((NJ, QUAD, nblk, SUB, group), BF16),
            vm((NJ, 2, nblk, SUB, group), BF16),
            vm((NJ, nblk, SUB, group), BF16),
            vm((NJ, planes, 2 * cap, SUB, group), BF16),
            vm((NJ, planes, 2 * cap, SUB, group), BF16),
            vm((NJ, planes, 2 * cap, SUB, group), BF16),
            pltpu.SMEM((shard_count * cap,), jnp.int32),
            dma((5,)),
            dma((planes, half)), dma((planes, half)), dma(()),
            dma((NJ, NI)), dma((NJ, NI, 2)), dma((NJ,)), dma((NJ, planes + 1)),
            dma((NJ,)), dma(()), dma((4,)), dma(()), dma((10,)),
        ],
        compiler_params=pltpu.CompilerParams(
            collective_id=0, has_side_effects=True, vmem_limit_bytes=54 * 2**20
        ),
    )(
        tokens, norm_gain[None, :], cotangent, key_bias[None, :],
        key_weight.reshape(cap, BLK, cols), block_slot,
    )
    return pl.pallas_call(
        write_kernel,
        out_shape=(
            jax.ShapeDtypeStruct((tok_count, cols), BF16),
            jax.ShapeDtypeStruct((tok_count, width), BF16),
            jax.ShapeDtypeStruct((cap, BLK, cols), F32),
            jax.ShapeDtypeStruct((1, width), F32),
            jax.ShapeDtypeStruct((1, cols), F32),
        ),
        in_specs=[local] * 4,
        out_specs=(hbm,) * 5,
        scratch_shapes=[vm((cap, BLK, cols), F32), dma((4,)), dma((cap,))],
        compiler_params=pltpu.CompilerParams(vmem_limit_bytes=8 * 2**20),
    )(*held)


def local(tokens, norm_gain, key_bias, key_weight, cotangent, block_slot):
    row_count, width = tokens.shape
    shard_count = lax.axis_size("shard")
    replicas = lax.axis_size("rep")
    grad_scale = float(row_count * shard_count * replicas) ** (-0.5)
    projected, token_grad, weight_grad, gain_grad, bias_grad = communicate(
        tokens, norm_gain, cotangent, key_bias, block_slot, key_weight, grad_scale
    )
    weight_grad = weight_grad.reshape(key_weight.shape)
    if replicas > QUAD:
        groups = [list(range(i, replicas, QUAD)) for i in range(QUAD)]
        weight_grad, gain_grad, bias_grad = lax.psum(
            (weight_grad, gain_grad, bias_grad), "rep", axis_index_groups=groups
        )
    return (projected, token_grad, weight_grad, gain_grad[0], bias_grad[0])


def solution(mesh):
    return jax.shard_map(
        local,
        mesh=mesh,
        in_specs=(
            P(("shard", "rep"), None),
            P(),
            P(),
            P("shard", None),
            P(("shard", "rep"), None),
            P(),
        ),
        out_specs=(
            P(("shard", "rep"), None),
            P(("shard", "rep"), None),
            P("shard", None),
            P(),
            P(),
        ),
        check_vma=False,
    )
```

time: 131 us -> 119 us (0.908)
  Pallas kernels: 131 us -> 118 us
    pallas_call x1, Pallas kernels: 127 us -> 114 us  [communicate(): pl.pallas_call(functools.partial(comm_kernel, planes, cap, nblk, scale),...]
where the time goes in v2:
time: 119 us
  Pallas kernels  118 us (99%)
    pallas_call x1, Pallas kernels, communicate(): pl.pallas_call(functools.partial(comm_kernel, planes, cap, nblk, scale),...  114 us
    pallas_call x1, Pallas kernels, communicate(): pl.pallas_call(write_kernel, out_shape=(jax.ShapeDtypeStruct((tok_count,...  3.6 us

profile of v2, /device:TPU:0, one launch (start us, length us, event | category | flops | bytes accessed | tf_op | source)
XLA Modules:
  0.0 118.7 jit_solution(14035262274791199525)
XLA Ops:
  0.6 114.3 %shard_map.101 = (bf16[384,1024]{1,0:T(8,128)(2,1)S(1)}, bf16[384,5120]{1,0:T(8,128)(2,1)S(1)}, bf16[8,8,8,16,128]{4,3,2,1,0:T(8,128)(2,1)S(1)}, f32[1,6144]{1,0:T(1,128)S(1)}) custom-call(bf16[384,5120]{1,0:T(8,128)(2,1)} %tok_h.1, f32[1,5120]{1,0:T(1,128)} %bitcast.7, bf16[384,1024]{1,0:T(8,128)(2,1)} %cot_h.1, f32[1,1024]{1,0:T(1,128)} %bitcast.8, ...), custom_call_target="tpu_custom_call" | custom-call | tf_op jit(solution)/shard_map/pallas_call | solution.py:565
  114.9 3.6 %shard_map.102 = (bf16[384,1024]{1,0:T(8,128)(2,1)}, bf16[384,5120]{1,0:T(8,128)(2,1)}, f32[8,128,1024]{2,1,0:T(8,128)}, f32[1,5120]{1,0:T(1,128)}, f32[1,1024]{1,0:T(1,128)}) custom-call(bf16[384,1024]{1,0:T(8,128)(2,1)S(1)} %get-tuple-element.14.proj, bf16[384,5120]{1,0:T(8,128)(2,1)S(1)} %get-tuple-element.15.tgrad, ...), custom_call_target="tpu_custom_call" | custom-call | tf_op jit(solution)/shard_map/pallas_call | solution.py:607

commit v3 on v2

--- a/solution.py
+++ b/solution.py
@@ -11,82 +11,108 @@
 NJ = 8
 NI = 4
 SUB = BLK // NJ
+HROW = BLK // 2
 QUAD = 4
 MESH = pl.DeviceIdType.MESH
 F32 = jnp.float32
 BF16 = jnp.bfloat16
 COMPUTE = 3
-FGRP = 8
-BGRP = 4
+BGRP = 8
 
 OWN, OWNP, SQ, TERM, SUM, HOP1, HOP2, PLACE, ZUP, ZDN, ZEND, PASS = range(12)
-FWD, BWD, AGZ, AGSIDE, AGPART, AGEND, G0, GSTEP, GEND, OWNER = range(12, 22)
+FWD, BWD, AGZ, AGSIDE, AGPART, G0, GSTEP, GEND, OWNER, RAW, OWNX = range(12, 23)
 COMMON = (SQ, TERM, FWD, BWD)
 
 TUNED = (
     (
-        (OWN, 0, 0), (OWN, 1, 0), (OWN, 2, 0), (OWN, 3, 0), (OWNP, 0, 0), (SQ, 0, 0), (TERM, 0, 0),
-        (TERM, 1, 0), (SUM, 0, 0), (HOP1, 0, 0), (SUM, 1, 0), (HOP1, 1, 0), (SUM, 3, 0), (SUM, 2, 0),
-        (SUM, 5, 0), (HOP1, 5, 0), (HOP1, 3, 0), (HOP1, 2, 0), (TERM, 2, 0), (AGZ, 1, 0), (AGSIDE, 1, 0),
-        (SUM, 4, 1), (SUM, 1, 1), (HOP2, 2, 0), (SUM, 1, 2), (HOP1, 1, 1), (SUM, 3, 1), (HOP1, 3, 1),
-        (SUM, 4, 0), (SUM, 5, 1), (TERM, 3, 0), (HOP1, 4, 1), (SUM, 7, 2), (HOP1, 5, 1), (HOP1, 7, 2),
-        (SUM, 0, 3), (SUM, 3, 2), (SUM, 0, 1), (HOP2, 0, 0), (SUM, 3, 3), (HOP1, 0, 3), (SUM, 2, 1),
-        (SUM, 5, 3), (AGZ, 1, 1), (SUM, 0, 2), (SUM, 2, 2), (SUM, 4, 3), (HOP2, 5, 0), (SUM, 6, 1),
-        (HOP2, 1, 0), (HOP1, 3, 3), (HOP1, 0, 1), (SUM, 1, 3), (SUM, 5, 2), (HOP1, 1, 3), (HOP1, 2, 1),
-        (HOP1, 4, 0), (HOP1, 4, 3), (HOP1, 3, 2), (SUM, 2, 3), (HOP1, 0, 2), (HOP1, 5, 3), (HOP2, 2, 1),
-        (SUM, 4, 2), (HOP2, 4, 0), (HOP1, 2, 2), (AGPART, 1, 0), (HOP2, 0, 1), (AGZ, 1, 2), (HOP1, 1, 2),
-        (HOP2, 3, 1), (HOP2, 3, 0), (HOP1, 2, 3), (HOP2, 0, 3), (AGSIDE, 1, 2), (SUM, 6, 2), (HOP1, 4, 2),
-        (AGSIDE, 1, 1), (HOP2, 3, 3), (SUM, 7, 3), (HOP2, 1, 1), (SUM, 6, 3), (HOP2, 1, 2), (HOP2, 4, 1),
-        (HOP2, 1, 3), (OWNER, 0, 0), (SUM, 7, 0), (HOP2, 5, 3), (AGZ, 2, 0), (HOP2, 2, 3), (HOP2, 0, 2),
-        (HOP2, 3, 2), (AGSIDE, 2, 0), (AGZ, 1, 3), (HOP2, 4, 3), (HOP2, 4, 2), (AGSIDE, 1, 3), (HOP2, 2, 2),
-        (SUM, 7, 1), (SUM, 6, 0), (PLACE, 0, 0), (HOP1, 7, 3), (PLACE, 1, 0), (ZUP, 0, 2), (AGZ, 2, 1),
-        (PLACE, 3, 0), (AGZ, 2, 2), (AGSIDE, 2, 1), (AGPART, 1, 3), (HOP1, 6, 0), (PLACE, 4, 0), (ZUP, 1, 2),
-        (ZUP, 0, 3), (AGSIDE, 2, 2), (HOP1, 5, 2), (AGZ, 2, 3), (PLACE, 2, 0), (ZUP, 4, 1), (AGSIDE, 2, 3),
-        (AGZ, 3, 0), (AGSIDE, 3, 0), (ZUP, 1, 3), (HOP2, 5, 2), (ZUP, 2, 2), (HOP1, 6, 3), (AGZ, 3, 2),
-        (ZUP, 3, 3), (AGSIDE, 3, 2), (ZUP, 4, 3), (HOP1, 7, 1), (ZUP, 3, 1), (AGPART, 1, 1), (AGPART, 2, 0),
-        (AGZ, 3, 1), (HOP2, 5, 1), (AGSIDE, 3, 1), (ZUP, 2, 3), (AGPART, 1, 2), (AGZ, 3, 3), (ZUP, 3, 2),
-        (HOP1, 6, 1), (AGSIDE, 3, 3), (HOP1, 7, 0), (AGPART, 3, 2), (HOP2, 6, 3), (HOP2, 6, 0), (PLACE, 5, 0),
-        (ZUP, 4, 2), (AGPART, 2, 2), (HOP1, 6, 2), (ZUP, 5, 1), (ZUP, 5, 3), (ZUP, 0, 1), (ZUP, 1, 1),
-        (HOP2, 7, 3), (AGPART, 3, 0), (AGPART, 2, 3), (AGPART, 3, 1), (ZUP, 2, 1), (AGPART, 2, 1), (HOP2, 6, 1),
-        (AGPART, 3, 3), (HOP2, 7, 1), (HOP2, 7, 2), (ZUP, 5, 2), (HOP2, 6, 2), (HOP2, 7, 0), (AGEND, 0, 0),
-        (FWD, 0, 0), (ZEND, 1, 0), (FWD, 1, 0), (ZEND, 2, 0), (PLACE, 6, 0), (ZUP, 6, 3), (PLACE, 7, 0),
-        (ZUP, 7, 3), (ZUP, 6, 2), (ZUP, 7, 1), (ZEND, 3, 0), (FWD, 2, 0), (ZUP, 7, 2), (PASS, 1, 0),
-        (BWD, 0, 0), (PASS, 2, 0), (ZEND, 4, 0), (ZEND, 0, 0), (ZUP, 6, 1), (BWD, 1, 0), (ZEND, 5, 0),
-        (BWD, 2, 0), (G0, 0, 0), (GSTEP, 0, 0), (ZEND, 6, 0), (PASS, 5, 0), (ZEND, 7, 0), (PASS, 4, 0),
-        (PASS, 3, 0), (GSTEP, 1, 0), (PASS, 6, 0), (PASS, 0, 0), (PASS, 7, 0), (GEND, 0, 0),
+        (OWN, 0, 0), (OWN, 1, 0), (OWN, 2, 0), (OWN, 3, 0), (OWN, 4, 0), (OWN, 5, 0), (OWN, 6, 0),
+        (OWN, 7, 0), (OWNP, 0, 0), (SQ, 0, 0), (TERM, 0, 0), (TERM, 1, 0), (SUM, 1, 0), (HOP1, 1, 0),
+        (SUM, 4, 0), (AGZ, 1, 0), (AGSIDE, 1, 0), (SUM, 3, 0), (TERM, 2, 0), (SUM, 2, 0), (SUM, 0, 0),
+        (SUM, 1, 1), (HOP1, 4, 0), (HOP1, 1, 1), (HOP1, 2, 0), (OWNX, 0, 7), (HOP1, 3, 0), (SUM, 5, 1),
+        (SUM, 6, 0), (SUM, 3, 1), (TERM, 3, 0), (HOP1, 5, 1), (SUM, 2, 1), (SUM, 6, 2), (SUM, 0, 2),
+        (SUM, 7, 0), (SUM, 4, 1), (SUM, 4, 2), (SUM, 3, 2), (SUM, 0, 3), (HOP1, 0, 0), (AGZ, 1, 2),
+        (SUM, 2, 3), (SUM, 3, 3), (HOP1, 0, 2), (SUM, 0, 1), (SUM, 5, 2), (AGZ, 1, 3), (HOP1, 2, 1),
+        (SUM, 1, 3), (HOP2, 1, 0), (SUM, 5, 0), (SUM, 1, 2), (HOP1, 3, 2), (HOP1, 3, 3), (SUM, 7, 3),
+        (HOP2, 0, 0), (HOP1, 4, 2), (SUM, 4, 3), (AGZ, 1, 4), (HOP1, 1, 3), (HOP1, 2, 3), (HOP1, 4, 3),
+        (AGSIDE, 1, 4), (HOP1, 0, 1), (SUM, 6, 1), (RAW, 7, 0), (OWNX, 0, 3), (HOP2, 2, 1), (SUM, 5, 3),
+        (HOP1, 5, 3), (AGZ, 1, 6), (AGZ, 1, 1), (HOP2, 2, 0), (AGSIDE, 1, 2), (AGZ, 1, 5), (HOP1, 4, 1),
+        (HOP1, 0, 3), (AGSIDE, 1, 6), (SUM, 6, 3), (RAW, 6, 0), (HOP2, 3, 0), (RAW, 6, 1), (SUM, 7, 1),
+        (HOP1, 1, 2), (AGPART, 1, 2), (HOP2, 5, 1), (SUM, 2, 2), (HOP1, 3, 1), (SUM, 7, 2), (HOP2, 5, 3),
+        (AGZ, 2, 6), (HOP2, 4, 0), (HOP2, 1, 1), (HOP2, 0, 2), (AGZ, 2, 1), (HOP2, 1, 3), (HOP2, 1, 2),
+        (AGSIDE, 1, 3), (RAW, 7, 2), (HOP2, 4, 1), (AGSIDE, 2, 6), (HOP2, 0, 3), (HOP2, 3, 1), (HOP2, 4, 3),
+        (AGSIDE, 1, 1), (HOP2, 4, 2), (OWNER, 0, 0), (HOP2, 3, 2), (AGZ, 1, 7), (AGPART, 1, 0), (HOP2, 2, 3),
+        (RAW, 6, 3), (RAW, 6, 2), (HOP2, 0, 1), (HOP1, 2, 2), (HOP1, 5, 0), (AGZ, 2, 5), (PLACE, 1, 0),
+        (ZUP, 1, 2), (HOP1, 5, 2), (AGSIDE, 2, 1), (FWD, 0, 0), (PLACE, 0, 0), (PLACE, 4, 0), (ZUP, 4, 3),
+        (AGSIDE, 1, 5), (HOP2, 3, 3), (AGPART, 1, 3), (AGZ, 2, 4), (HOP2, 5, 2), (AGZ, 2, 3), (ZUP, 0, 3),
+        (HOP2, 2, 2), (AGZ, 3, 2), (AGZ, 2, 0), (AGZ, 2, 2), (AGPART, 1, 4), (RAW, 7, 3), (AGSIDE, 1, 7),
+        (AGSIDE, 2, 3), (PLACE, 3, 0), (AGZ, 2, 7), (AGSIDE, 2, 5), (AGSIDE, 2, 7), (HOP2, 5, 0), (AGSIDE, 3, 2),
+        (AGSIDE, 2, 0), (AGPART, 2, 6), (AGPART, 1, 7), (AGZ, 3, 7), (ZUP, 1, 3), (AGSIDE, 3, 7), (PLACE, 5, 0),
+        (ZUP, 3, 3), (RAW, 7, 1), (PLACE, 2, 0), (AGPART, 2, 1), (AGPART, 1, 5), (AGPART, 2, 7), (AGSIDE, 2, 2),
+        (AGZ, 3, 0), (AGZ, 3, 5), (ZUP, 5, 3), (ZUP, 0, 1), (AGSIDE, 3, 5), (AGZ, 3, 1), (AGSIDE, 3, 0),
+        (AGPART, 3, 7), (AGSIDE, 2, 4), (AGSIDE, 3, 1), (ZUP, 0, 2), (AGZ, 3, 3), (AGPART, 2, 5), (ZUP, 1, 1),
+        (ZUP, 2, 3), (AGPART, 2, 2), (AGPART, 1, 1), (AGPART, 3, 2), (ZUP, 2, 2), (AGSIDE, 3, 3), (AGPART, 1, 6),
+        (ZUP, 3, 2), (AGZ, 3, 6), (AGSIDE, 3, 6), (AGZ, 3, 4), (AGSIDE, 3, 4), (AGPART, 2, 0), (AGPART, 3, 5),
+        (AGPART, 2, 3), (AGPART, 2, 4), (ZUP, 4, 2), (FWD, 1, 0), (AGPART, 3, 1), (ZUP, 2, 1), (ZUP, 5, 2),
+        (ZEND, 1, 0), (FWD, 2, 0), (AGPART, 3, 6), (AGPART, 3, 3), (AGPART, 3, 0), (ZEND, 4, 0), (ZUP, 3, 1),
+        (AGPART, 3, 4), (ZEND, 0, 0), (ZUP, 5, 1), (ZEND, 3, 0), (ZUP, 4, 1), (FWD, 3, 0), (PASS, 4, 0),
+        (ZEND, 5, 0), (BWD, 0, 0), (PASS, 0, 0), (PASS, 1, 0), (PASS, 3, 0), (BWD, 1, 0), (ZEND, 2, 0),
+        (BWD, 2, 0), (G0, 0, 0), (GSTEP, 0, 0), (ZEND, 6, 0), (PASS, 5, 0), (ZEND, 7, 0), (PASS, 2, 0),
+        (GSTEP, 1, 0), (PASS, 7, 0), (PASS, 6, 0), (GEND, 0, 0),
     ),
     (
-        (OWN, 0, 0), (OWN, 1, 0), (OWN, 2, 0), (OWN, 3, 0), (OWNP, 0, 0), (SQ, 0, 0), (TERM, 0, 0),
-        (TERM, 1, 0), (SUM, 0, 0), (SUM, 3, 0), (SUM, 2, 0), (HOP1, 2, 0), (SUM, 1, 0), (HOP1, 3, 0),
-        (HOP1, 1, 0), (HOP1, 0, 0), (TERM, 2, 0), (SUM, 1, 1), (HOP1, 1, 1), (SUM, 0, 1), (SUM, 3, 1),
-        (AGZ, 2, 0), (SUM, 4, 1), (AGSIDE, 2, 0), (HOP2, 0, 0), (SUM, 7, 1), (SUM, 3, 2), (SUM, 1, 2),
-        (HOP1, 4, 1), (HOP1, 1, 2), (AGZ, 0, 0), (HOP1, 7, 1), (SUM, 6, 1), (AGSIDE, 0, 0), (SUM, 5, 2),
-        (AGZ, 2, 1), (HOP1, 3, 1), (HOP2, 4, 1), (HOP1, 3, 2), (SUM, 0, 2), (AGZ, 2, 2), (AGSIDE, 2, 2),
-        (TERM, 3, 0), (AGSIDE, 2, 1), (AGZ, 2, 3), (SUM, 0, 3), (HOP1, 0, 3), (HOP2, 1, 0), (AGZ, 0, 1),
-        (HOP1, 0, 2), (SUM, 1, 3), (HOP1, 1, 3), (AGZ, 0, 2), (AGSIDE, 0, 2), (AGZ, 0, 3), (AGSIDE, 0, 1),
-        (SUM, 2, 1), (AGSIDE, 0, 3), (HOP2, 3, 2), (SUM, 7, 0), (SUM, 7, 3), (HOP2, 1, 3), (AGPART, 2, 1),
-        (HOP2, 1, 1), (SUM, 6, 0), (HOP1, 0, 1), (SUM, 4, 0), (AGZ, 3, 0), (HOP1, 7, 3), (SUM, 2, 3),
-        (SUM, 6, 2), (SUM, 5, 0), (SUM, 5, 3), (HOP2, 0, 2), (HOP1, 6, 2), (HOP2, 0, 3), (SUM, 2, 2),
-        (AGSIDE, 2, 3), (SUM, 7, 2), (AGZ, 3, 2), (AGPART, 0, 2), (SUM, 3, 3), (HOP2, 3, 1), (HOP2, 0, 1),
-        (AGZ, 3, 1), (AGSIDE, 3, 0), (AGSIDE, 3, 1), (AGSIDE, 3, 2), (AGZ, 3, 3), (HOP2, 1, 2), (HOP1, 2, 2),
-        (AGSIDE, 3, 3), (AGPART, 2, 0), (OWNER, 0, 0), (AGPART, 3, 2), (AGPART, 3, 0), (HOP2, 3, 0), (AGPART, 3, 1),
-        (AGPART, 0, 1), (HOP1, 2, 3), (AGPART, 0, 0), (SUM, 4, 2), (AGPART, 0, 3), (PLACE, 1, 0), (HOP2, 2, 0),
-        (HOP1, 2, 1), (ZUP, 1, 3), (HOP1, 3, 3), (SUM, 5, 1), (SUM, 4, 3), (AGPART, 3, 3), (HOP1, 4, 2),
-        (PLACE, 0, 0), (HOP1, 5, 0), (AGPART, 2, 3), (HOP2, 2, 3), (HOP2, 2, 2), (HOP2, 7, 3), (HOP2, 3, 3),
-        (HOP2, 2, 1), (HOP1, 5, 2), (HOP1, 4, 0), (ZUP, 0, 2), (SUM, 6, 3), (ZUP, 0, 3), (HOP1, 5, 3),
-        (HOP1, 5, 1), (AGPART, 2, 2), (HOP1, 4, 3), (AGEND, 0, 0), (FWD, 0, 0), (HOP2, 4, 0), (HOP1, 6, 1),
-        (ZUP, 1, 2), (PLACE, 3, 0), (ZUP, 3, 3), (HOP1, 6, 3), (HOP2, 4, 2), (FWD, 1, 0), (ZDN, 1, 0),
-        (HOP2, 4, 3), (HOP2, 5, 0), (ZUP, 3, 2), (ZDN, 0, 0), (PLACE, 2, 0), (ZUP, 2, 3), (FWD, 2, 0),
-        (HOP1, 7, 2), (HOP1, 7, 0), (HOP2, 5, 1), (HOP2, 6, 1), (HOP2, 6, 2), (HOP2, 5, 3), (ZDN, 3, 0),
-        (HOP2, 5, 2), (BWD, 0, 0), (HOP2, 7, 1), (HOP2, 6, 3), (PLACE, 4, 0), (ZDN, 2, 0), (ZEND, 0, 0),
-        (ZUP, 4, 3), (PLACE, 5, 0), (HOP1, 6, 0), (ZEND, 1, 0), (ZUP, 4, 2), (ZUP, 5, 3), (ZDN, 4, 0),
-        (ZUP, 2, 2), (BWD, 1, 0), (HOP2, 7, 0), (ZUP, 5, 2), (HOP2, 7, 2), (HOP2, 6, 0), (ZEND, 3, 0),
-        (ZDN, 5, 0), (ZEND, 4, 0), (BWD, 2, 0), (G0, 0, 0), (PLACE, 6, 0), (ZUP, 6, 3), (PASS, 1, 0),
-        (PLACE, 7, 0), (ZEND, 5, 0), (ZUP, 7, 3), (ZUP, 6, 2), (PASS, 0, 0), (ZDN, 6, 0), (ZEND, 2, 0),
-        (GSTEP, 0, 0), (PASS, 4, 0), (PASS, 3, 0), (ZUP, 7, 2), (ZDN, 7, 0), (ZEND, 6, 0), (PASS, 5, 0),
-        (ZEND, 7, 0), (GSTEP, 1, 0), (PASS, 6, 0), (PASS, 7, 0), (PASS, 2, 0), (GEND, 0, 0),
+        (OWN, 0, 0), (OWN, 1, 0), (OWN, 2, 0), (OWN, 3, 0), (OWN, 4, 0), (OWN, 5, 0), (OWN, 6, 0),
+        (OWN, 7, 0), (OWNP, 0, 0), (SQ, 0, 0), (TERM, 0, 0), (TERM, 1, 0), (SUM, 0, 0), (SUM, 1, 0),
+        (HOP1, 0, 0), (HOP1, 1, 0), (SUM, 3, 0), (AGZ, 0, 0), (TERM, 2, 0), (SUM, 5, 0), (HOP1, 5, 0),
+        (SUM, 4, 0), (SUM, 3, 1), (AGSIDE, 0, 0), (SUM, 5, 1), (SUM, 2, 0), (HOP1, 3, 0), (SUM, 5, 2),
+        (SUM, 0, 1), (SUM, 1, 1), (HOP1, 1, 1), (HOP2, 1, 0), (HOP1, 2, 0), (HOP1, 0, 1), (SUM, 2, 1),
+        (AGZ, 0, 2), (SUM, 1, 2), (HOP2, 0, 0), (AGSIDE, 0, 2), (AGZ, 0, 1), (HOP1, 3, 1), (SUM, 2, 2),
+        (OWNX, 0, 6), (TERM, 3, 0), (HOP1, 5, 1), (HOP2, 2, 0), (HOP1, 4, 0), (SUM, 4, 2), (SUM, 4, 3),
+        (SUM, 0, 3), (HOP1, 1, 2), (OWNER, 0, 0), (HOP1, 5, 2), (SUM, 3, 2), (HOP1, 0, 3), (HOP1, 3, 2),
+        (AGZ, 2, 1), (HOP1, 4, 2), (HOP1, 4, 3), (AGZ, 2, 6), (AGZ, 0, 3), (HOP2, 3, 0), (SUM, 5, 3),
+        (AGZ, 2, 3), (SUM, 2, 3), (HOP2, 5, 0), (SUM, 4, 1), (HOP1, 5, 3), (AGZ, 0, 4), (AGSIDE, 0, 1),
+        (AGZ, 0, 5), (FWD, 1, 0), (AGZ, 2, 0), (OWNX, 0, 3), (HOP1, 4, 1), (HOP1, 2, 3), (AGZ, 0, 7),
+        (SUM, 1, 3), (HOP2, 5, 2), (HOP2, 5, 1), (HOP1, 1, 3), (AGZ, 2, 2), (AGZ, 0, 6), (AGSIDE, 0, 5),
+        (HOP2, 3, 2), (HOP1, 2, 2), (AGSIDE, 0, 4), (SUM, 7, 0), (HOP2, 5, 3), (AGZ, 2, 5), (AGPART, 0, 0),
+        (AGZ, 3, 2), (AGZ, 2, 4), (AGZ, 2, 7), (AGSIDE, 2, 5), (AGSIDE, 0, 6), (SUM, 3, 3), (AGPART, 2, 6),
+        (HOP2, 1, 2), (HOP2, 0, 3), (SUM, 6, 0), (HOP2, 2, 3), (HOP2, 4, 0), (AGPART, 0, 4), (HOP1, 3, 3),
+        (SUM, 0, 2), (OWNX, 0, 7), (AGSIDE, 2, 4), (AGSIDE, 2, 0), (HOP1, 2, 1), (SUM, 6, 1), (HOP2, 4, 2),
+        (HOP1, 0, 2), (PLACE, 5, 0), (SUM, 7, 2), (AGZ, 3, 5), (HOP2, 4, 1), (AGSIDE, 2, 1), (HOP2, 4, 3),
+        (HOP2, 0, 1), (AGPART, 0, 7), (AGSIDE, 3, 5), (AGPART, 0, 6), (OWNX, 0, 2), (HOP1, 6, 0), (HOP1, 7, 0),
+        (AGPART, 0, 1), (SUM, 6, 3), (AGZ, 3, 7), (HOP2, 1, 1), (HOP2, 0, 2), (HOP2, 1, 3), (HOP2, 2, 1),
+        (AGPART, 2, 0), (HOP2, 3, 3), (SUM, 6, 2), (AGZ, 3, 0), (AGSIDE, 3, 7), (AGZ, 3, 1), (PLACE, 4, 0),
+        (AGZ, 3, 6), (HOP1, 6, 2), (AGSIDE, 3, 6), (HOP2, 3, 1), (HOP1, 6, 1), (HOP2, 2, 2), (AGPART, 2, 3),
+        (AGZ, 3, 3), (AGPART, 2, 4), (AGPART, 0, 5), (ZUP, 4, 3), (PLACE, 0, 0), (ZUP, 0, 3), (AGSIDE, 3, 2),
+        (AGPART, 3, 5), (AGPART, 2, 2), (HOP1, 6, 3), (HOP2, 6, 1), (PLACE, 1, 0), (AGPART, 0, 2), (AGPART, 2, 7),
+        (AGZ, 3, 4), (AGPART, 2, 5), (ZUP, 1, 3), (HOP2, 6, 2), (PLACE, 3, 0), (AGSIDE, 3, 0), (AGPART, 2, 1),
+        (AGPART, 0, 3), (ZDN, 1, 0), (ZUP, 1, 2), (AGSIDE, 3, 4), (AGPART, 3, 7), (HOP2, 6, 0), (PLACE, 2, 0),
+        (AGSIDE, 3, 1), (FWD, 2, 0), (AGPART, 3, 0), (HOP1, 7, 2), (AGSIDE, 3, 3), (SUM, 7, 3), (ZDN, 0, 0),
+        (ZUP, 3, 3), (FWD, 0, 0), (ZDN, 4, 0), (ZUP, 5, 3), (HOP2, 6, 3), (AGPART, 3, 1), (ZUP, 0, 2),
+        (HOP1, 7, 3), (ZDN, 3, 0), (AGPART, 3, 2), (AGPART, 3, 6), (AGPART, 3, 4), (HOP2, 7, 0), (HOP2, 7, 2),
+        (SUM, 7, 1), (HOP1, 7, 1), (ZUP, 2, 3), (AGPART, 3, 3), (PLACE, 6, 0), (ZEND, 1, 0), (ZDN, 5, 0),
+        (ZUP, 2, 2), (ZEND, 0, 0), (ZUP, 6, 2), (FWD, 3, 0), (ZUP, 3, 2), (HOP2, 7, 3), (HOP2, 7, 1),
+        (ZUP, 6, 3), (BWD, 0, 0), (ZEND, 2, 0), (ZDN, 2, 0), (ZUP, 4, 2), (ZEND, 6, 0), (BWD, 1, 0),
+        (PASS, 0, 0), (PLACE, 7, 0), (ZEND, 3, 0), (PASS, 1, 0), (ZDN, 6, 0), (ZUP, 7, 3), (ZUP, 7, 2),
+        (BWD, 2, 0), (G0, 0, 0), (ZEND, 4, 0), (ZUP, 5, 2), (ZDN, 7, 0), (GSTEP, 0, 0), (ZEND, 7, 0),
+        (ZEND, 5, 0), (PASS, 6, 0), (GSTEP, 1, 0), (PASS, 3, 0), (PASS, 4, 0), (PASS, 7, 0), (PASS, 2, 0),
+        (PASS, 5, 0), (GEND, 0, 0),
     ),
 )
+
+
+MOVED = (6, 7)
+DIRECT = {(0, 1): (), (1, 0): (7, 3), (1, 2): (7, 3, 6, 2)}
+
+
+def moved_of(planes, cap):
+    return MOVED if planes == 4 and cap == 8 else ()
+
+
+def direct_of(to, of, planes, cap):
+    if planes != 4 or cap != 8:
+        return ()
+    if 2 * to >= planes:
+        to, of = planes - 1 - to, planes - 1 - of
+    return DIRECT.get((to, of), ())
 
 
 def mirror(order, planes):
@@ -95,14 +121,16 @@
     for step, a, b in order:
         if step in (ZUP, ZDN):
             b = planes - 1 - b
-        if step in (AGZ, AGSIDE, AGPART):
+        if step in (AGZ, AGSIDE, AGPART, FWD):
             a = planes - 1 - a
+        if step == OWNX:
+            a = 1 - a
         out.append((flip.get(step, step), a, b))
     return out
 
 
 def plain_order(z, planes, cap):
-    half = cap // 2
+    half = cap
     out = [(OWN, k, 0) for k in range(half)] + [(OWNP, 0, 0), (SQ, 0, 0), (OWNER, 0, 0)]
     out += [(TERM, i, 0) for i in range(NI)]
     for step in (SUM, HOP1, HOP2):
@@ -121,9 +149,8 @@
                 out.append((ZDN, j, t))
     for step in (ZEND, PASS):
         out += [(step, j, 0) for j in range(NJ)]
-    out.append((AGEND, 0, 0))
-    for step in (FWD, BWD):
-        out += [(step, g, 0) for g in range(COMPUTE)]
+    out += [(FWD, q, 0) for q in range(planes)]
+    out += [(BWD, g, 0) for g in range(COMPUTE)]
     out.append((G0, 0, 0))
     out += [(GSTEP, n, 0) for n in range(2)]
     out.append((GEND, 0, 0))
@@ -137,14 +164,17 @@
 
 
 def split(order):
-    parts, common = [[]], []
+    parts, common, gathered = [[]], [], []
     for tok in order:
         if tok[0] in COMMON:
+            if tok[0] == FWD:
+                gathered.append(tok[1])
+                tok = (FWD, len(gathered) - 1, 0)
             common.append(tok)
             parts.append([])
         else:
             parts[-1].append(tok)
-    return parts, common
+    return parts, common, gathered
 
 
 def comm_kernel(
@@ -152,8 +182,8 @@
     tok_h, gain_h, cot_h, bias_h, w_h, slot_of,
     proj, tgrad, frecv, vec,
     whole, tok, cot, gain, bias, inv, coef, fwd, gst, grecv, gz,
-    part, drecv, r1, r2, slots, zup, zdn, bos,
-    in_sem, agz_r, ags_r, agp_r, d_r, r1_r, r2_r, z_r, pass_r, end_r, g_r, gz_r, sent,
+    part, drecv, r1, r2, raw, slots, zup, zdn, bos,
+    in_sem, agz_r, ags_r, agp_r, d_r, r1_r, r2_r, raw_r, z_r, pass_r, end_r, g_r, gz_r, sent,
 ):
     s = lax.axis_index("shard")
     r = lax.axis_index("rep")
@@ -206,8 +236,9 @@
             src_ref=src, dst_ref=dst, send_sem=ss, recv_sem=rs, device_id=dev, device_id_type=MESH
         )
 
-    half = cap // 2
-    quar = cap // 4
+    moved = moved_of(planes, cap)
+    half = cap
+    quar = cap // 2
     hh = (x + y) % 2
     tokens_here, width = tok.shape
     wide = 5 * BLK
@@ -215,8 +246,8 @@
     per_plane = 2 * cap
 
     def held(q, core, which, k):
-        start = hh * half if which == 0 else (1 - hh) * half
-        return whole.at[pl.ds((2 * q + core) * cap + start + k, 1)]
+        start = (hh if which == 0 else 1 - hh) * (cap // 2) + k // 2
+        return whole.at[pl.ds((2 * q + core) * cap + start, 1), pl.ds(k % 2 * HROW, HROW)]
 
     def ag_z(q, d, k):
         ref = held(q, c, 0, k)
@@ -226,16 +257,23 @@
         ref = held(q, c, which, k)
         return rdma(ref, ref, sent.at[1], ags_r.at[q, k], xdev if k < quar else ydev)
 
+    def ag_direct(zz, d, k):
+        ref = held(zz, c, 1, k)
+        return rdma(ref, ref, sent.at[0], ags_r.at[zz, k], updev if d == 0 else dndev)
+
+    def direct(to, of):
+        return direct_of(to, of, planes, cap) if 0 <= to < planes and 0 <= of < planes else ()
+
     def ag_part(q, which, k):
         ref = held(q, c, which, k)
-        return rdma(ref, ref, sent.at[2], agp_r, partner)
+        return rdma(ref, ref, sent.at[2], agp_r.at[q], partner)
 
     def own_part():
         ref = whole.at[pl.ds(s * cap, cap)]
-        return rdma(ref, ref, sent.at[2], agp_r, partner)
-
-    def slots_of(count, ss, rs):
-        ref = whole.at[pl.ds(0, count)]
+        return rdma(ref, ref, sent.at[2], agp_r.at[z], partner)
+
+    def chunks_of(count, ss, rs):
+        ref = whole.at[pl.ds(0, count), pl.ds(0, HROW)]
         return rdma(ref, ref, ss, rs, partner)
 
     def onward(zz, q):
@@ -265,6 +303,14 @@
         blocks = pl.ds(i * nb, nb)
         return rdma(
             part.at[c, j, far, blocks], r2.at[j, blocks], sent.at[5], r2_r.at[j], dev
+        )
+
+    def raw_copy(zz, j, i):
+        blocks = pl.ds(i * nb, nb)
+        m = moved.index(j)
+        return rdma(
+            part.at[c, j, :, blocks], raw.at[m, :, blocks], sent.at[10], raw_r.at[m, i],
+            updev if zz == 0 else dndev,
         )
 
     def add_to(dst, src, start, count):
@@ -338,8 +384,8 @@
         )
         res = (res * scale).astype(BF16)
         group = res.shape[1] // (2 * QUAD)
-        tgrad[:, cols] = normed
         for b in range(wide // BLK):
+            tgrad[i * (wide // BLK) + b] = normed[:, b * BLK:(b + 1) * BLK]
             for j in range(NJ):
                 lo = b * BLK + j * SUB
                 for k in range(QUAD):
@@ -355,11 +401,17 @@
         groups = nblk // grp
         return groups * a // COMPUTE, groups * (a + 1) // COMPUTE
 
-    def fwd_body(g, carry):
-        gw = FGRP * BLK
-        cols = pl.ds(pl.multiple_of(g * gw, gw), gw)
-        fwd[...] += jnp.dot(tgrad[:, cols], weight_group(g, FGRP), preferred_element_type=F32)
-        return carry
+    def fwd_body(q, core):
+        first = (2 * q + core) * cap
+        cols = []
+        for u in range(cap):
+            b = bos[first + u]
+            val = tgrad[jnp.maximum(b, 0)]
+            cols.append(jnp.where(b >= 0, val.astype(F32), 0.0).astype(BF16))
+        rows = whole[pl.ds(first, cap)].reshape(cap * BLK, whole.shape[2])
+        fwd[...] += jnp.dot(
+            jnp.concatenate(cols, axis=1), rows, preferred_element_type=F32
+        )
 
     def bwd_body(g, carry):
         gw = BGRP * BLK
@@ -369,7 +421,9 @@
         )
         values = tok[:, cols].astype(F32)
         grad = grad * inv[...]
-        tgrad[:, cols] = (grad * gain[:, cols] - values * coef[...]).astype(BF16)
+        out = (grad * gain[:, cols] - values * coef[...]).astype(BF16)
+        for b in range(BGRP):
+            tgrad[g * BGRP + b] = out[:, b * BLK:(b + 1) * BLK]
         gst[0, :, cols] = jnp.sum(grad * values, axis=0, keepdims=True) * scale
         return carry
 
@@ -380,7 +434,7 @@
                 0, width // (2 * BLK), squares, jnp.zeros((tokens_here, BLK), F32)
             )
             inv[...] = lax.rsqrt(jnp.sum(acc, axis=1, keepdims=True) / width + EPS)
-            for cp in loads[2:]:
+            for cp in loads[2:5]:
                 cp.wait()
         elif step == TERM:
             count = width // wide
@@ -390,7 +444,14 @@
         elif step == FWD:
             if a == 0:
                 fwd[...] = jnp.zeros_like(fwd)
-            lax.fori_loop(*cuts(FGRP, a), fwd_body, 0)
+            q = sum(jnp.where(z == zz, plans[zz][2][a], 0) for zz in range(planes))
+            chunks_of(2 * cap, sent.at[2], agp_r.at[q]).wait_recv()
+
+            def body(core, carry):
+                fwd_body(q, core)
+                return carry
+
+            lax.fori_loop(0, 2, body, 0)
         else:
             if a == 0:
                 total = fwd[...]
@@ -400,6 +461,9 @@
                 gst[0, :, width:] = jnp.sum(cot[...].astype(F32), axis=0, keepdims=True) * scale
             lax.fori_loop(*cuts(BGRP, a), bwd_body, 0)
 
+    ends = (0, planes - 1)
+    beside = (1, planes - 2)
+
     def own_step(zz, step, a, b):
         if step == OWN:
             for d in onward(zz, zz):
@@ -408,6 +472,10 @@
             own_part().start()
         elif step == OWNER:
             lax.fori_loop(0, 2 * planes * cap, owner, 0)
+        elif step == OWNX:
+            ag_direct(zz, a, b).start()
+        elif step == RAW:
+            raw_copy(zz, a, b).start()
         elif step == AGZ:
             ag_z(a, 0, b).wait_recv()
             for d in onward(zz, a):
@@ -418,12 +486,14 @@
         elif step == AGPART:
             ag_side(a, 1, b).wait_recv()
             ag_part(a, 1, b).start()
-        elif step == AGEND:
-            slots_of(planes * cap, sent.at[2], agp_r).wait_recv()
         elif step == SUM:
             d_copy(a, b).wait_recv()
             for k in range(QUAD):
                 add_to(part.at[c, a, k], drecv.at[a, k], b * nb, nb)
+            if a in moved and zz in beside:
+                raw_copy(zz, a, b).wait_recv()
+                for k in range(QUAD):
+                    add_to(part.at[c, a, k], raw.at[moved.index(a), k], b * nb, nb)
         elif step == HOP1:
             first_hop(a, b, 1).start()
             first_hop(a, b, 0).start()
@@ -447,22 +517,24 @@
 
             lax.fori_loop(0, planes, body, 0)
         elif step == ZUP:
-            if zz > 0:
+            if zz > (1 if a in moved else 0):
                 z_copy(a, b, True, zz).wait_recv()
                 add_to(slots.at[a, b], zup.at[a, b], 0, per_plane)
             z_copy(a, b, True, zz).start()
         elif step == ZDN:
-            if zz < planes - 1:
+            if zz < planes - (2 if a in moved else 1):
                 z_copy(a, b, False, zz).wait_recv()
                 add_to(slots.at[a, b], zdn.at[a, b], 0, per_plane)
             z_copy(a, b, False, zz - 1).start()
         elif step == ZEND:
-            if zz > 0:
-                z_copy(a, zz, True, zz).wait_recv()
-                add_to(slots.at[a, zz], zup.at[a, zz], 0, per_plane)
-            if zz < planes - 1:
-                z_copy(a, zz, False, zz).wait_recv()
-                add_to(slots.at[a, zz], zdn.at[a, zz], 0, per_plane)
+            for up, buf in ((True, zup), (False, zdn)):
+                hops = zz if up else planes - 1 - zz
+                if hops > (1 if a in moved else 0) or (a in moved and hops == planes - 1):
+                    z_copy(a, zz, up, zz).wait_recv()
+                    if a in moved and zz in ends:
+                        slots[a, zz] = buf[a, zz]
+                    else:
+                        add_to(slots.at[a, zz], buf.at[a, zz], 0, per_plane)
             for cp in f_copies(zz, a):
                 cp.start()
             frecv[a, my_id] = slots[a, zz, pl.ds(c * cap, cap)]
@@ -494,15 +566,21 @@
     def finish(zz):
         f_all(sent.at[8], end_r, 5).wait_recv()
         count = sum(len(onward(zz, q)) for q in range(planes)) * half
-        slots_of(count, sent.at[0], agp_r).wait_send()
-        slots_of((planes - 1) * half, sent.at[1], agp_r).wait_send()
-        slots_of(planes * cap, sent.at[2], agp_r).wait_send()
+        count += len(direct(zz + 1, zz)) + len(direct(zz - 1, zz))
+        chunks_of(count, sent.at[0], end_r).wait_send()
+        count = (planes - 1) * half - len(direct(zz, zz - 1)) - len(direct(zz, zz + 1))
+        chunks_of(count, sent.at[1], end_r).wait_send()
+        chunks_of(2 * planes * cap, sent.at[2], end_r).wait_send()
         rdma(drecv, drecv, sent.at[3], end_r, partner).wait_send()
-        rdma(r1, r1, sent.at[4], end_r, partner).wait_send()
-        rdma(r2, r2, sent.at[5], end_r, partner).wait_send()
+        pieces = NJ - (len(moved) if zz in ends else 0)
+        for n, buf in ((4, r1), (5, r2)):
+            ref = buf.at[pl.ds(0, pieces)]
+            rdma(ref, ref, sent.at[n], end_r, partner).wait_send()
+        if pieces < NJ:
+            rdma(raw, raw, sent.at[10], end_r, partner).wait_send()
         for n, count in ((6, planes - 1 - zz), (7, zz)):
             if count:
-                ref = slots.at[:, pl.ds(0, count)]
+                ref = slots.at[pl.ds(0, pieces), pl.ds(0, count)]
                 rdma(ref, ref, sent.at[n], end_r, partner).wait_send()
         f_all(sent.at[8], end_r, 7).wait_send()
         g_all(gz.at[pl.ds(0, planes - 1)], sent.at[9], gz_r).wait_send()
@@ -527,14 +605,15 @@
             shared_step(*common[n][:2])
 
 
-def write_kernel(proj, tgrad, frecv, vec, proj_h, tgrad_h, wgrad_h, gain_h, bias_h, buf, sem, wsem):
+def write_kernel(proj, tgrad, frecv, vec, proj_h, tgrad_h, wgrad_h, gain_h, bias_h, buf, sem):
     width = gain_h.shape[1]
     cap = frecv.shape[2]
+    for b in range(tgrad.shape[0]):
+        pltpu.make_async_copy(tgrad.at[b], tgrad_h.at[:, pl.ds(b * BLK, BLK)], sem.at[3]).start()
     copies = [
-        pltpu.make_async_copy(tgrad, tgrad_h, sem.at[0]),
-        pltpu.make_async_copy(proj, proj_h, sem.at[1]),
-        pltpu.make_async_copy(vec.at[:, :width], gain_h, sem.at[2]),
-        pltpu.make_async_copy(vec.at[:, width:], bias_h, sem.at[3]),
+        pltpu.make_async_copy(proj, proj_h, sem.at[0]),
+        pltpu.make_async_copy(vec.at[:, :width], gain_h, sem.at[1]),
+        pltpu.make_async_copy(vec.at[:, width:], bias_h, sem.at[2]),
     ]
     for cp in copies:
         cp.start()
@@ -542,11 +621,11 @@
         for j in range(NJ):
             for n in range(2 * QUAD):
                 buf[u, j * SUB:(j + 1) * SUB, n * BLK:(n + 1) * BLK] = frecv[j, n, u].astype(F32)
-        cp = pltpu.make_async_copy(buf.at[u], wgrad_h.at[u], wsem.at[u])
-        cp.start()
-        copies.append(cp)
+        pltpu.make_async_copy(buf.at[u], wgrad_h.at[u], sem.at[4]).start()
     for cp in copies:
         cp.wait()
+    pltpu.make_async_copy(tgrad_h, tgrad_h, sem.at[3]).wait()
+    pltpu.make_async_copy(buf, wgrad_h, sem.at[4]).wait()
 
 
 def communicate(tokens, norm_gain, cotangent, key_bias, block_slot, key_weight, scale):
@@ -554,7 +633,7 @@
     planes = shard_count // 2
     rows, cols = key_weight.shape
     cap = rows // BLK
-    half = cap // 2
+    raws = max(1, len(moved_of(planes, cap)))
     tok_count, width = tokens.shape
     nblk = width // BLK
     group = cols // (2 * QUAD)
@@ -566,11 +645,11 @@
         functools.partial(comm_kernel, planes, cap, nblk, scale),
         out_shape=(
             vm((tok_count, cols), BF16),
-            vm((tok_count, width), BF16),
+            vm((nblk, tok_count, BLK), BF16),
             vm((NJ, 2 * QUAD, cap, SUB, group), BF16),
             vm((1, width + cols), F32),
         ),
-        in_specs=[hbm, hbm, hbm, hbm, hbm, pl.BlockSpec(memory_space=pltpu.SMEM)],
+        in_specs=[hbm] * 5 + [pl.BlockSpec(memory_space=pltpu.SMEM)],
         out_specs=(local,) * 4,
         scratch_shapes=[
             vm((shard_count * cap, BLK, cols), BF16),
@@ -588,14 +667,15 @@
             vm((NJ, QUAD, nblk, SUB, group), BF16),
             vm((NJ, 2, nblk, SUB, group), BF16),
             vm((NJ, nblk, SUB, group), BF16),
+            vm((raws, QUAD, nblk, SUB, group), BF16),
             vm((NJ, planes, 2 * cap, SUB, group), BF16),
             vm((NJ, planes, 2 * cap, SUB, group), BF16),
             vm((NJ, planes, 2 * cap, SUB, group), BF16),
             pltpu.SMEM((shard_count * cap,), jnp.int32),
             dma((5,)),
-            dma((planes, half)), dma((planes, half)), dma(()),
-            dma((NJ, NI)), dma((NJ, NI, 2)), dma((NJ,)), dma((NJ, planes + 1)),
-            dma((NJ,)), dma(()), dma((4,)), dma(()), dma((10,)),
+            dma((planes, cap)), dma((planes, cap)), dma((planes,)),
+            dma((NJ, NI)), dma((NJ, NI, 2)), dma((NJ,)), dma((raws, NI)), dma((NJ, planes + 1)),
+            dma((NJ,)), dma(()), dma((4,)), dma(()), dma((11,)),
         ],
         compiler_params=pltpu.CompilerParams(
             collective_id=0, has_side_effects=True, vmem_limit_bytes=54 * 2**20
@@ -615,7 +695,7 @@
         ),
         in_specs=[local] * 4,
         out_specs=(hbm,) * 5,
-        scratch_shapes=[vm((cap, BLK, cols), F32), dma((4,)), dma((cap,))],
+        scratch_shapes=[vm((cap, BLK, cols), F32), dma((5,))],
         compiler_params=pltpu.CompilerParams(vmem_limit_bytes=8 * 2**20),
     )(*held)
 

time: 119 us -> 109 us (0.916)
  Pallas kernels: 118 us -> 108 us
    pallas_call x1, Pallas kernels: 114 us -> 104 us  [communicate(): pl.pallas_call(functools.partial(comm_kernel, planes, cap, nblk, scale),...]
where the time goes in v3:
time: 109 us
  Pallas kernels  108 us (99%)
    pallas_call x1, Pallas kernels, communicate(): pl.pallas_call(functools.partial(comm_kernel, planes, cap, nblk, scale),...  104 us
    pallas_call x1, Pallas kernels, communicate(): pl.pallas_call(write_kernel, out_shape=(jax.ShapeDtypeStruct((tok_count,...  3.5 us

profile of v3, /device:TPU:0, one launch (start us, length us, event | category | flops | bytes accessed | tf_op | source)
XLA Modules:
  0.0 108.7 jit_solution(4060838472590591635)
XLA Ops:
  0.6 104.4 %shard_map.101 = (bf16[384,1024]{1,0:T(8,128)(2,1)S(1)}, bf16[40,384,128]{2,1,0:T(8,128)(2,1)S(1)}, bf16[8,8,8,16,128]{4,3,2,1,0:T(8,128)(2,1)S(1)}, f32[1,6144]{1,0:T(1,128)S(1)}) custom-call(bf16[384,5120]{1,0:T(8,128)(2,1)} %tok_h.1, f32[1,5120]{1,0:T(1,128)} %bitcast.7, bf16[384,1024]{1,0:T(8,128)(2,1)} %cot_h.1, f32[1,1024]{1,0:T(1,128)} %bitcast.8, ...), custom_call_target="tpu_custom_call" | custom-call | tf_op jit(solution)/shard_map/pallas_call | solution.py:644
  105.0 3.5 %shard_map.102 = (bf16[384,1024]{1,0:T(8,128)(2,1)}, bf16[384,5120]{1,0:T(8,128)(2,1)}, f32[8,128,1024]{2,1,0:T(8,128)}, f32[1,5120]{1,0:T(1,128)}, f32[1,1024]{1,0:T(1,128)}) custom-call(bf16[384,1024]{1,0:T(8,128)(2,1)S(1)} %get-tuple-element.14.proj, bf16[40,384,128]{2,1,0:T(8,128)(2,1)S(1)} %get-tuple-element.15.tgrad, ...), custom_call_target="tpu_custom_call" | custom-call | tf_op jit(solution)/shard_map/pallas_call | solution.py:687
